TPU v7x, 512 devices: a whole 4x4x16 slice. The times are simulated.
512 devices in a mesh: grp: 8 (over y_lo, x), shard: 64 (over z, y_hi, core).
Axes of the slice: x: 4, y: 4 (y_hi: 2, y_lo: 2; y = y_hi * 2 + y_lo), z: 16, core: 2. Of those that a mesh axis runs over, the one named last changes fastest.
Arguments:
- window: bfloat16 [128, 4096], P('grp'), may hold values from -6 to 6
- weight: bfloat16 [11008, 4096], P('shard'), may hold values from -0.09375 to 0.09375
- factor_a: bfloat16 [1024, 4, 4096], P(('grp', 'shard')), may hold values from -6 to 6
- factor_b: bfloat16 [1024, 4, 11008], P(('grp', 'shard')), may hold values from -6 to 6
- fitness: float32 [1024], P(('grp', 'shard')), may hold values from -4 to 4
Outputs:
- perturbed: bfloat16 [11008, 16384], P('shard', 'grp')
- update: float32 [11008, 4096], P('shard', 'grp')
All inputs are finite; a program needn't handle non-finite values.
Results may differ from a plain program's by a relative error of at most 0.0029.
Values may be sent and summed in bfloat16 or wider, within the bound.
No kernel may reach another device: no remote copies, remote signals or barrier semaphores. Data moves between devices by JAX's collectives and lax.ppermute only.
A program may use at most 64 MiB of HBM per device.

v0:
```python
import functools
import math

import jax
import jax.numpy as jnp
from jax import lax
from jax.experimental import pallas as pl
from jax.experimental.pallas import tpu as pltpu
from jax.sharding import Mesh
from jax.sharding import PartitionSpec as P


F32, BF16 = jnp.float32, jnp.bfloat16
Q = ("yhi", "core")
SHARD = ("z", "yhi", "core")
GRP_SHARD = ("grp", "z", "yhi", "core")
LANE = 128
PARTS = 3
NT = (((1,), (1,)), ((), ()))


def up8(n):
    return (n + 7) // 8 * 8


def upl(n):
    return (n + LANE - 1) // LANE * LANE


def call(body, out_shape, args, flops, scratch=(), smem=()):
    vmem = pl.BlockSpec(memory_space=pltpu.VMEM)
    scalar = pl.BlockSpec(memory_space=pltpu.SMEM)
    many = isinstance(out_shape, (list, tuple))
    return pl.pallas_call(
        body,
        out_shape=out_shape,
        in_specs=[scalar if i in smem else vmem for i in range(len(args))],
        out_specs=[vmem] * len(out_shape) if many else vmem,
        scratch_shapes=list(scratch),
        cost_estimate=pl.CostEstimate(flops=flops, bytes_accessed=1 << 20, transcendentals=0),
        compiler_params=pltpu.CompilerParams(vmem_limit_bytes=40 << 20),
    )(*args)


def split3(x):
    hi = x.astype(BF16).astype(F32)
    rest = x - hi
    mid = rest.astype(BF16).astype(F32)
    return hi, mid, (rest - mid).astype(BF16).astype(F32)


def cut_a(a_ref, out_ref):
    groups, _, width = out_ref.shape
    cands = a_ref.shape[0]
    for g in range(groups):
        columns = slice(g * width, (g + 1) * width)
        both = [a_ref[c, :, columns].astype(F32) for c in range(cands)]
        out_ref[g] = jnp.concatenate(both, axis=0).astype(BF16)


def pack_b(fit_ref, win_ref, a_ref, b_ref, out_ref, wide_ref):
    nz, rows, lanes = out_ref.shape
    cands, rank, hidden = b_ref.shape
    tok, depth = win_ref.shape
    nq = 4
    own = hidden // (nz * nq)
    step = up8(own)
    for c in range(cands):
        wide_ref[c * rank : (c + 1) * rank, :hidden] = b_ref[c].astype(F32)
    wide_ref[:, hidden:] = jnp.zeros((rows, wide_ref.shape[1] - hidden), F32)
    a_rows = jnp.concatenate([a_ref[c].astype(F32) for c in range(cands)], axis=0).astype(BF16)
    first = nq * step % LANE
    win = win_ref[...]
    spread = jnp.concatenate(
        [jnp.zeros((first, depth), BF16)]
        + [win] * PARTS
        + [jnp.zeros((LANE - first - PARTS * tok, depth), BF16)],
        axis=0,
    )
    proj = lax.dot_general(a_rows, spread, NT, preferred_element_type=F32)
    lane = lax.broadcasted_iota(jnp.int32, (rows, LANE), 1)
    row = lax.broadcasted_iota(jnp.int32, (rows, LANE), 0)
    hi, mid, lo = split3(proj)
    extra = jnp.where(lane < first + tok, hi, jnp.where(lane < first + 2 * tok, mid, lo))
    fit = jnp.where(row < rank, fit_ref[0], fit_ref[1])
    fhi, fmid, flo = split3(fit)
    at = first + PARTS * tok
    fits = jnp.where(lane == at, fhi, jnp.where(lane == at + 1, fmid, flo))
    extra = jnp.where(lane < at, extra, jnp.where(lane < at + 3, fits, 0.0))
    for z in range(nz):
        block = [jnp.zeros((rows, LANE), F32) for _ in range(lanes // LANE)]
        for q in range(nq):
            source = (z * nq + q) * own
            base = source // LANE * LANE
            target = q * step
            start = target // LANE
            offset = target % LANE
            span = min(3, len(block) - start)
            window = wide_ref[:, base : base + 3 * LANE]
            turn = (offset - (source - base)) % (3 * LANE)
            if turn:
                window = pltpu.roll(window, turn, 1)
            for k in range(span):
                at_lane = lane + k * LANE
                inside = (at_lane >= offset) & (at_lane < offset + own)
                piece = window[:, k * LANE : (k + 1) * LANE]
                block[start + k] = jnp.where(inside, piece, block[start + k])
        block[-1] = jnp.where(lane >= first, extra, block[-1])
        out_ref[z] = jnp.concatenate(block, axis=1).astype(BF16)


def turn_b(in_ref, w_ref, p_ref):
    nz, rows, lanes = in_ref.shape
    nq, tall, _ = p_ref.shape
    hidden = w_ref.shape[1]
    step = hidden // nq
    proj = tall - step
    x = in_ref[...].astype(F32).reshape(nz * rows, lanes).T
    at = hidden + proj
    fit = x[at : at + 1] + (x[at + 1 : at + 2] + x[at + 2 : at + 3])
    b = x[:hidden]
    weighted = (b * fit).astype(BF16)
    for g in range(w_ref.shape[0]):
        w_ref[g] = weighted
    b = b.astype(BF16)
    extra = x[hidden:at].astype(BF16)
    for q in range(nq):
        p_ref[q, :step] = b[q * step : (q + 1) * step]
        p_ref[q, step:] = extra


def base_rows(weight_ref, win_ref, out_ref):
    tok = win_ref.shape[0]
    spread = jnp.concatenate([win_ref[...]] * (LANE // tok), axis=0)
    out_ref[...] = lax.dot_general(weight_ref[...], spread, NT, preferred_element_type=F32)


def perturb(scale, in_ref, base_ref, out_ref):
    nq, tall, lanes = in_ref.shape
    own = base_ref.shape[0]
    step = up8(own)
    tok = (tall - step) // PARTS
    rank = 4
    wide = nq * lanes
    x = jnp.concatenate([in_ref[q] for q in range(nq)], axis=1)
    source = lax.broadcasted_iota(jnp.int32, (wide, wide), 0)
    target = lax.broadcasted_iota(jnp.int32, (wide, wide), 1)
    place = ((source & 127) >> 3) * 32 + (source >> 7) * 8 + (source & 7)
    move = jnp.where(place == target, 1.0, 0.0).astype(BF16)
    x = jnp.dot(x, move, preferred_element_type=F32)
    cands = LANE // rank
    n = lax.broadcasted_iota(jnp.int32, (cands * tok, PARTS * LANE), 0)
    k = lax.broadcasted_iota(jnp.int32, (cands * tok, PARTS * LANE), 1)
    same = (n // tok) == ((k & 127) >> 2)
    base = jnp.concatenate([base_ref[...]] * (cands * tok // LANE), axis=1)
    for part in range(wide // LANE):
        tile = x[:, part * LANE : (part + 1) * LANE]
        b = tile[:step].astype(BF16)
        left = jnp.concatenate([b] * PARTS, axis=1)
        proj = jnp.concatenate(
            [tile[step + i * tok : step + (i + 1) * tok] for i in range(PARTS)], axis=1
        )
        right = jnp.where(same, jnp.concatenate([proj] * cands, axis=0), 0.0).astype(BF16)
        low = lax.dot_general(left, right, NT, preferred_element_type=F32)
        out = base + scale * low[:own]
        out_ref[:, part * cands * tok : (part + 1) * cands * tok] = out.astype(BF16)


OFFSETS = ((0, 5, -5), (1, 6, -4), (-1, 4, -6), (2, 7, -3), (-2, 3, -7))


def update_parts(*refs):
    at_ref, w_ref = refs[:2]
    chunks, (first_ref, second_ref) = refs[2:7], refs[7:9]
    out_refs = refs[9:13]
    rows_ref, sum_ref = refs[13:]
    groups, nz, rows, width = rows_ref.shape
    z = at_ref[0]
    for ref, offsets in zip(chunks, OFFSETS):
        for i, offset in enumerate(offsets):
            place = lax.rem(z + offset + nz, nz)
            for g in range(groups):
                rows_ref[g, place] = ref[i, g]
    place = lax.rem(z + nz // 2, nz)
    for g in range(groups // 2):
        rows_ref[g, place] = first_ref[g]
        rows_ref[groups // 2 + g, place] = second_ref[g]
    left = jnp.concatenate([w_ref[g] for g in range(groups)], axis=1)
    right = rows_ref[...].reshape(groups * nz * rows, width)
    sum_ref[...] = jnp.dot(left, right, preferred_element_type=F32)
    y, core = at_ref[1], at_ref[2]
    tall = out_refs[0].shape[0]
    for ref, yy, cc in zip(out_refs, (y, y, 1 - y, 1 - y), (core, 1 - core, core, 1 - core)):
        start = pl.multiple_of((yy * 2 + cc) * tall, 8)
        ref[...] = sum_ref[pl.ds(start, tall), :]


def shifted(value, offset):
    n = lax.axis_size("z")
    return lax.ppermute(value, "z", [(i, (i - offset) % n) for i in range(n)])


def swapped(value, axis):
    return lax.ppermute(value, axis, [(0, 1), (1, 0)])


def exchanged(value, axis):
    return lax.all_to_all(value, axis, 0, 0, tiled=True)


def step(window, weight, factor_a, factor_b, fitness):
    tok, depth = window.shape
    own = weight.shape[0]
    cands, rank, hidden = factor_b.shape
    groups, nz = lax.axis_size("grp"), lax.axis_size("z")
    nq = 4
    total = cands * groups * nz * nq
    rows = cands * rank
    width = depth // groups
    block = up8(own)
    lanes = upl(nq * block + PARTS * tok + 3)
    shape = jax.ShapeDtypeStruct

    cut = call(cut_a, shape((groups, rows, width), BF16), (factor_a,), 1 << 20)
    mine = exchanged(cut, "grp")

    packed = call(
        pack_b,
        shape((nz, rows, lanes), BF16),
        (fitness, window, factor_a, factor_b),
        1 << 24,
        scratch=[pltpu.VMEM((rows, upl(hidden) + 2 * LANE), F32)],
        smem=(0,),
    )
    columns = exchanged(packed, "z")
    weighted, pieces = call(
        turn_b,
        [
            shape((groups, nq * block, nz * rows), BF16),
            shape((nq, block + PARTS * tok, nz * rows), BF16),
        ],
        (columns,),
        1 << 24,
    )
    weighted = exchanged(weighted, "grp")
    pieces = exchanged(pieces, Q)
    base = call(base_rows, shape((own, LANE), F32), (weight, window), 1 << 28)
    perturbed = call(
        functools.partial(perturb, 0.25 / math.sqrt(depth)),
        shape((own, cands * nz * nq * tok), BF16),
        (pieces, base),
        1 << 30,
    )

    mine = mine[None]
    near = jnp.concatenate([mine, shifted(mine, 5), shifted(mine, -5)], axis=0)
    up, down = shifted(near, 1), shifted(near, -1)
    up2, down2 = shifted(up, 1), shifted(down, -1)
    half = groups // 2
    first = shifted(up[1, :half], 2)
    second = shifted(down[2, half:], -2)
    at = jnp.stack([lax.axis_index("z"), lax.axis_index("yhi"), lax.axis_index("core")])
    part = shape((block, width), F32)
    oo, ox, xo, xx = call(
        update_parts,
        [part] * 4,
        (at.astype(jnp.int32), weighted, near, up, down, up2, down2, first, second),
        1 << 30,
        scratch=[
            pltpu.VMEM((groups, nz, rows, width), BF16),
            pltpu.VMEM((nq * block, width), F32),
        ],
        smem=(0,),
    )
    there = xo + swapped(xx, "core")
    here = oo + swapped(ox, "core")
    update = (here + swapped(there, "yhi"))[:own] * (0.5 / math.sqrt(total))
    return perturbed, update


def solution(mesh):
    split = Mesh(
        mesh.devices.reshape(mesh.shape["grp"], mesh.shape["shard"] // 4, 2, 2), GRP_SHARD
    )
    return jax.shard_map(
        step,
        mesh=split,
        in_specs=(
            P("grp", None),
            P(SHARD, None),
            P(GRP_SHARD, None, None),
            P(GRP_SHARD, None, None),
            P(GRP_SHARD),
        ),
        out_specs=(P(SHARD, "grp"), P(SHARD, "grp")),
        check_vma=False,
    )
```

profile of v0, /device:TPU:34, one launch (start us, length us, event | category | flops | bytes accessed | tf_op | source)
XLA Modules:
  0.0 122.4 jit_solution(8112096723620966994)
XLA Ops:
  0.6 0.0 copy-start.1
  0.6 0.9 copy-done.1
  1.5 0.0 copy-start.3
  1.5 0.8 copy-done.3
  2.4 0.0 copy-start.5
  2.4 0.9 copy-done.5
  3.3 0.0 copy-start.6
  3.3 0.7 copy-done.6
  4.0 1.6 %shard_map.68 = bf16[16,8,768]{2,1,0:T(8,128)(2,1)} custom-call(f32[2]{0:T(128)S(1)} %copy-done.6, bf16[16,4096]{1,0:T(8,128)(2,1)S(1)} %copy-done.1, bf16[2,4,4096]{2,1,0:T(4,128)(2,1)S(1)} %copy-done.3, bf16[2,4,11008]{2,1,0:T(4,128)(2,1)S(1)} %copy-done.5), custom_call_target="tpu_custom_call" | custom-call | flops 16777216 | bytes 1048576 | tf_op jit(solution)/shard_map/pallas_call | solution.py:34
  5.6 15.2 %all-to-all-start = ((bf16[16,8,768]{2,1,0:T(8,128)(2,1)}), bf16[16,8,768]{2,1,0:T(8,128)(2,1)S(1)}, u32[]{:S(2)}, u32[]{:S(2)}) async-start(bf16[16,8,768]{2,1,0:T(8,128)(2,1)} %shard_map.68), calls=%async_computation | async-start | bytes 393216 | tf_op jit(solution)/shard_map/all_to_all | solution.py:208
  20.8 0.0 copy-start.4
  20.8 0.8 copy-done.4
  21.6 0.6 shard_map.72
  22.3 14.4 %all-to-all-done.in_ref = bf16[16,8,768]{2,1,0:T(8,128)(2,1)S(1)} async-done(((bf16[16,8,768]{2,1,0:T(8,128)(2,1)}), bf16[16,8,768]{2,1,0:T(8,128)(2,1)S(1)}, u32[]{:S(2)}, u32[]{:S(2)}) %all-to-all-start) | async-done | bytes 196640 | tf_op jit(solution)/shard_map/all_to_all | solution.py:208
  36.7 5.8 %all-to-all-start.3 = ((bf16[8,8,512]{2,1,0:T(8,128)(2,1)}), bf16[8,8,512]{2,1,0:T(8,128)(2,1)S(1)}, u32[]{:S(2)}, u32[]{:S(2)}) async-start(bf16[8,8,512]{2,1,0:T(8,128)(2,1)} %shard_map.72), calls=%async_computation.3 | async-start | bytes 131072 | tf_op jit(solution)/shard_map/all_to_all | solution.py:208
  42.5 1.4 %shard_map.69 = (bf16[8,704,128]{2,1,0:T(8,128)(2,1)}, bf16[4,224,128]{2,1,0:T(8,128)(2,1)}) custom-call(bf16[16,8,768]{2,1,0:T(8,128)(2,1)S(1)} %all-to-all-done.in_ref), custom_call_target="tpu_custom_call" | custom-call | flops 16777216 | bytes 1048576 | tf_op jit(solution)/shard_map/pallas_call | solution.py:34
  43.9 3.7 %all-to-all-done.3 = bf16[8,8,512]{2,1,0:T(8,128)(2,1)S(1)} async-done(((bf16[8,8,512]{2,1,0:T(8,128)(2,1)}), bf16[8,8,512]{2,1,0:T(8,128)(2,1)S(1)}, u32[]{:S(2)}, u32[]{:S(2)}) %all-to-all-start.3) | async-done | bytes 65568 | tf_op jit(solution)/shard_map/all_to_all | solution.py:208
  47.6 4.8 %all-to-all-start.2 = ((bf16[8,704,128]{2,1,0:T(8,128)(2,1)}), bf16[8,704,128]{2,1,0:T(8,128)(2,1)S(1)}, u32[]{:S(2)}, u32[]{:S(2)}) async-start(bf16[8,704,128]{2,1,0:T(8,128)(2,1)} %get-tuple-element.9), calls=%async_computation.2 | async-start | bytes 2883584 | tf_op jit(solution)/shard_map/all_to_all | solution.py:208
  52.4 4.8 %collective-permute-start = (bf16[1,8,8,512]{3,2,1,0:T(8,128)(2,1)S(1)}, bf16[1,8,8,512]{3,2,1,0:T(8,128)(2,1)S(1)}, u32[]{:S(2)}, u32[]{:S(2)}) collective-permute-start(bf16[1,8,8,512]{3,2,1,0:T(8,128)(2,1)S(1)} %bitcast.8), channel_id=1, source_target_pairs={{0,44},{4,48},{8,52},{12,56},{16,60},{20,0},{24,4},{28,8},{32,12},... | collective-permute-start | bytes 196616 | tf_op jit(solution)/shard_map/ppermute | solution.py:200
  57.1 5.9 %collective-permute-start.1 = (bf16[1,8,8,512]{3,2,1,0:T(8,128)(2,1)S(1)}, bf16[1,8,8,512]{3,2,1,0:T(8,128)(2,1)S(1)}, u32[]{:S(2)}, u32[]{:S(2)}) collective-permute-start(bf16[1,8,8,512]{3,2,1,0:T(8,128)(2,1)S(1)} %bitcast.9), channel_id=1, source_target_pairs={{0,20},{4,24},{8,28},{12,32},{16,36},{20,40},{24,44},{28,48},{32,5... | collective-permute-start | bytes 196616 | tf_op jit(solution)/shard_map/ppermute | solution.py:200
  63.0 0.3 collective-permute-done
  63.3 6.0 %collective-permute-done.1 = bf16[1,8,8,512]{3,2,1,0:T(8,128)(2,1)S(1)} collective-permute-done((bf16[1,8,8,512]{3,2,1,0:T(8,128)(2,1)S(1)}, bf16[1,8,8,512]{3,2,1,0:T(8,128)(2,1)S(1)}, u32[]{:S(2)}, u32[]{:S(2)}) %collective-permute-start.1) | collective-permute-done | bytes 65568 | tf_op jit(solution)/shard_map/ppermute | solution.py:200
  69.3 4.6 %collective-permute-start.2 = (bf16[3,8,8,512]{3,2,1,0:T(8,128)(2,1)S(1)}, bf16[3,8,8,512]{3,2,1,0:T(8,128)(2,1)S(1)}, u32[]{:S(2)}, u32[]{:S(2)}) collective-permute-start(bf16[3,8,8,512]{3,2,1,0:T(8,128)(2,1)S(1)} %pad_maximum_fusion.refs_2_), channel_id=1, source_target_pairs={{0,60},{4,0},{8,4},{12,8},{16,12},{20,16},{24,20},{28,24},{32,28},... | collective-permute-start | bytes 589832 | tf_op jit(solution)/shard_map/ppermute | solution.py:200
  73.9 1.9 %collective-permute-start.3 = (bf16[3,8,8,512]{3,2,1,0:T(8,128)(2,1)S(1)}, bf16[3,8,8,512]{3,2,1,0:T(8,128)(2,1)S(1)}, u32[]{:S(2)}, u32[]{:S(2)}) collective-permute-start(bf16[3,8,8,512]{3,2,1,0:T(8,128)(2,1)S(1)} %pad_maximum_fusion.refs_2_), channel_id=1, source_target_pairs={{0,4},{4,8},{8,12},{12,16},{16,20},{20,24},{24,28},{28,32},{32,36}... | collective-permute-start | bytes 589832 | tf_op jit(solution)/shard_map/ppermute | solution.py:200
  75.8 1.9 %collective-permute-done.2.refs_3_ = bf16[3,8,8,512]{3,2,1,0:T(8,128)(2,1)S(1)} collective-permute-done((bf16[3,8,8,512]{3,2,1,0:T(8,128)(2,1)S(1)}, bf16[3,8,8,512]{3,2,1,0:T(8,128)(2,1)S(1)}, u32[]{:S(2)}, u32[]{:S(2)}) %collective-permute-start.2) | collective-permute-done | bytes 196640 | tf_op jit(solution)/shard_map/ppermute | solution.py:200
  77.8 4.7 %collective-permute-start.6 = (bf16[4,8,512]{2,1,0:T(8,128)(2,1)S(1)}, bf16[4,8,512]{2,1,0:T(8,128)(2,1)S(1)}, u32[]{:S(2)}, u32[]{:S(2)}) collective-permute-start(bf16[4,8,512]{2,1,0:T(8,128)(2,1)S(1)} %slice_bitcast_fusion.1), channel_id=1, source_target_pairs={{0,56},{4,60},{8,0},{12,4},{16,8},{20,12},{24,16},{28,20},{32,24},... | collective-permute-start | bytes 98312 | tf_op jit(solution)/shard_map/ppermute | solution.py:200
  82.5 1.9 %collective-permute-start.4 = (bf16[3,8,8,512]{3,2,1,0:T(8,128)(2,1)S(1)}, bf16[3,8,8,512]{3,2,1,0:T(8,128)(2,1)S(1)}, u32[]{:S(2)}, u32[]{:S(2)}) collective-permute-start(bf16[3,8,8,512]{3,2,1,0:T(8,128)(2,1)S(1)} %collective-permute-done.2.refs_3_), channel_id=1, source_target_pairs={{0,60},{4,0},{8,4},{12,8},{16,12},{20,16},{24,20},{28,24},{32,28},... | collective-permute-start | bytes 589832 | tf_op jit(solution)/shard_map/ppermute | solution.py:200
  84.4 0.0 collective-permute-done.3.refs_4_
  84.4 3.9 %collective-permute-start.5 = (bf16[3,8,8,512]{3,2,1,0:T(8,128)(2,1)S(1)}, bf16[3,8,8,512]{3,2,1,0:T(8,128)(2,1)S(1)}, u32[]{:S(2)}, u32[]{:S(2)}) collective-permute-start(bf16[3,8,8,512]{3,2,1,0:T(8,128)(2,1)S(1)} %collective-permute-done.3.refs_4_), channel_id=1, source_target_pairs={{0,4},{4,8},{8,12},{12,16},{16,20},{20,24},{24,28},{28,32},{32,36}... | collective-permute-start | bytes 589832 | tf_op jit(solution)/shard_map/ppermute | solution.py:200
  88.3 6.2 %collective-permute-start.7 = (bf16[4,8,512]{2,1,0:T(8,128)(2,1)S(1)}, bf16[4,8,512]{2,1,0:T(8,128)(2,1)S(1)}, u32[]{:S(2)}, u32[]{:S(2)}) collective-permute-start(bf16[4,8,512]{2,1,0:T(8,128)(2,1)S(1)} %slice_bitcast_fusion), channel_id=1, source_target_pairs={{0,8},{4,12},{8,16},{12,20},{16,24},{20,28},{24,32},{28,36},{32,40... | collective-permute-start | bytes 98312 | tf_op jit(solution)/shard_map/ppermute | solution.py:200
  94.5 0.1 pad_add_fusion.refs_0_
  94.6 0.0 collective-permute-done.6.refs_7_
  94.6 1.6 %collective-permute-done.7.refs_8_ = bf16[4,8,512]{2,1,0:T(8,128)(2,1)S(1)} collective-permute-done((bf16[4,8,512]{2,1,0:T(8,128)(2,1)S(1)}, bf16[4,8,512]{2,1,0:T(8,128)(2,1)S(1)}, u32[]{:S(2)}, u32[]{:S(2)}) %collective-permute-start.7) | collective-permute-done | bytes 32800 | tf_op jit(solution)/shard_map/ppermute | solution.py:200
  96.3 0.0 collective-permute-done.4.refs_5_
  96.3 0.0 collective-permute-done.5.refs_6_
  96.3 0.0 all-to-all-done.2.refs_1_
  96.3 0.0 copy-start.2
  96.3 1.6 %shard_map.73 = (f32[176,512]{1,0:T(8,128)S(1)}, f32[176,512]{1,0:T(8,128)S(1)}, f32[176,512]{1,0:T(8,128)S(1)}, f32[176,512]{1,0:T(8,128)S(1)}) custom-call(s32[3]{0:T(128)S(1)} %pad_add_fusion.refs_0_, bf16[8,704,128]{2,1,0:T(8,128)(2,1)S(1)} %all-to-all-done.2.refs_1_, bf16[3,8,8,512]{3,2,1,0:T(8,128)(2,1)S(1)} %pad_maximum_fusion.refs_2_, ...), custom_call_target="tpu_custom_call" | custom-call | flops 1073741824 | bytes 1048576 | tf_op jit(solution)/shard_map/pallas_call | solution.py:34
  97.9 0.0 copy-start
  97.9 2.1 %collective-permute-start.9 = (f32[176,512]{1,0:T(8,128)S(1)}, f32[176,512]{1,0:T(8,128)S(1)}, u32[]{:S(2)}, u32[]{:S(2)}) collective-permute-start(f32[176,512]{1,0:T(8,128)S(1)} %get-tuple-element.13), channel_id=1, source_target_pairs={{0,1},{1,0},{2,3},{3,2},{4,5},{5,4},{6,7},{7,6},{8,9},{9,8},{10,11... | collective-permute-start | bytes 1081352 | tf_op jit(solution)/shard_map/ppermute | solution.py:204
  100.0 2.4 %collective-permute-start.8 = (f32[176,512]{1,0:T(8,128)S(1)}, f32[176,512]{1,0:T(8,128)}, u32[]{:S(2)}, u32[]{:S(2)}) collective-permute-start(f32[176,512]{1,0:T(8,128)S(1)} %get-tuple-element.11), channel_id=1, source_target_pairs={{0,1},{1,0},{2,3},{3,2},{4,5},{5,4},{6,7},{7,6},{8,9},{9,8},{10,11... | collective-permute-start | bytes 1081352 | tf_op jit(solution)/shard_map/ppermute | solution.py:204
  102.4 0.0 collective-permute-done.9
  102.4 0.1 add.10
  102.5 4.8 %collective-permute-start.10 = (f32[176,512]{1,0:T(8,128)S(1)}, f32[176,512]{1,0:T(8,128)}, u32[]{:S(2)}, u32[]{:S(2)}) collective-permute-start(f32[176,512]{1,0:T(8,128)S(1)} %add.10), channel_id=1, source_target_pairs={{0,2},{2,0},{1,3},{3,1},{4,6},{6,4},{5,7},{7,5},{8,10},{10,8},{9,1... | collective-permute-start | bytes 1081352 | tf_op jit(solution)/shard_map/ppermute | solution.py:204
  107.3 3.4 %all-to-all-start.1 = ((bf16[4,224,128]{2,1,0:T(8,128)(2,1)}), bf16[4,224,128]{2,1,0:T(8,128)(2,1)S(1)}, u32[]{:S(2)}, u32[]{:S(2)}) async-start(bf16[4,224,128]{2,1,0:T(8,128)(2,1)} %get-tuple-element.8), calls=%async_computation.1 | async-start | bytes 458752 | tf_op jit(solution)/shard_map/all_to_all | solution.py:208
  110.7 0.0 copy-done.2
  110.7 0.0 copy-done
  110.7 0.5 shard_map.70.base_ref
  111.3 7.4 %all-to-all-done.1.in_ref = bf16[4,224,128]{2,1,0:T(8,128)(2,1)S(1)} async-done(((bf16[4,224,128]{2,1,0:T(8,128)(2,1)}), bf16[4,224,128]{2,1,0:T(8,128)(2,1)S(1)}, u32[]{:S(2)}, u32[]{:S(2)}) %all-to-all-start.1) | async-done | bytes 229408 | tf_op jit(solution)/shard_map/all_to_all | solution.py:208
  118.7 1.9 %shard_map.71 = bf16[172,2048]{1,0:T(8,128)(2,1)} custom-call(bf16[4,224,128]{2,1,0:T(8,128)(2,1)S(1)} %all-to-all-done.1.in_ref, f32[172,128]{1,0:T(8,128)S(1)} %shard_map.70.base_ref), custom_call_target="tpu_custom_call" | custom-call | flops 1073741824 | bytes 1048576 | tf_op jit(solution)/shard_map/pallas_call | solution.py:34
  120.5 0.0 collective-permute-done.8
  120.5 0.0 collective-permute-done.10
  120.5 1.9 %fusion = f32[172,512]{1,0:T(8,128)} fusion(f32[176,512]{1,0:T(8,128)} %collective-permute-done.10, f32[176,512]{1,0:T(8,128)} %collective-permute-done.8, f32[176,512]{1,0:T(8,128)S(1)} %get-tuple-element.10), kind=kLoop, calls=%fused_computation.1 | loop fusion | flops 264192 | bytes 1409024 | tf_op jit(solution)/shard_map/mul | solution.py:277
  (3 shorter events, 0.0 us)
Async XLA Ops:
  0.6 0.9 copy-start.1
  1.5 0.8 copy-start.3
  2.4 0.9 copy-start.5
  3.3 0.7 copy-start.6
  5.6 31.1 %all-to-all-start = ((bf16[16,8,768]{2,1,0:T(8,128)(2,1)}), bf16[16,8,768]{2,1,0:T(8,128)(2,1)S(1)}, u32[]{:S(2)}, u32[]{:S(2)}) async-start(bf16[16,8,768]{2,1,0:T(8,128)(2,1)} %shard_map.68), calls=%async_computation | async-start | bytes 393216 | tf_op jit(solution)/shard_map/all_to_all | solution.py:208
  20.8 0.8 copy-start.4
  36.7 10.9 %all-to-all-start.3 = ((bf16[8,8,512]{2,1,0:T(8,128)(2,1)}), bf16[8,8,512]{2,1,0:T(8,128)(2,1)S(1)}, u32[]{:S(2)}, u32[]{:S(2)}) async-start(bf16[8,8,512]{2,1,0:T(8,128)(2,1)} %shard_map.72), calls=%async_computation.3 | async-start | bytes 131072 | tf_op jit(solution)/shard_map/all_to_all | solution.py:208
  47.6 48.7 %all-to-all-start.2 = ((bf16[8,704,128]{2,1,0:T(8,128)(2,1)}), bf16[8,704,128]{2,1,0:T(8,128)(2,1)S(1)}, u32[]{:S(2)}, u32[]{:S(2)}) async-start(bf16[8,704,128]{2,1,0:T(8,128)(2,1)} %get-tuple-element.9), calls=%async_computation.2 | async-start | bytes 2883584 | tf_op jit(solution)/shard_map/all_to_all | solution.py:208
  52.4 11.0 %collective-permute-start = (bf16[1,8,8,512]{3,2,1,0:T(8,128)(2,1)S(1)}, bf16[1,8,8,512]{3,2,1,0:T(8,128)(2,1)S(1)}, u32[]{:S(2)}, u32[]{:S(2)}) collective-permute-start(bf16[1,8,8,512]{3,2,1,0:T(8,128)(2,1)S(1)} %bitcast.8), channel_id=1, source_target_pairs={{0,44},{4,48},{8,52},{12,56},{16,60},{20,0},{24,4},{28,8},{32,12},... | collective-permute-start | bytes 196616 | tf_op jit(solution)/shard_map/ppermute | solution.py:200
  57.1 12.1 %collective-permute-start.1 = (bf16[1,8,8,512]{3,2,1,0:T(8,128)(2,1)S(1)}, bf16[1,8,8,512]{3,2,1,0:T(8,128)(2,1)S(1)}, u32[]{:S(2)}, u32[]{:S(2)}) collective-permute-start(bf16[1,8,8,512]{3,2,1,0:T(8,128)(2,1)S(1)} %bitcast.9), channel_id=1, source_target_pairs={{0,20},{4,24},{8,28},{12,32},{16,36},{20,40},{24,44},{28,48},{32,5... | collective-permute-start | bytes 196616 | tf_op jit(solution)/shard_map/ppermute | solution.py:200
  69.3 8.5 %collective-permute-start.2 = (bf16[3,8,8,512]{3,2,1,0:T(8,128)(2,1)S(1)}, bf16[3,8,8,512]{3,2,1,0:T(8,128)(2,1)S(1)}, u32[]{:S(2)}, u32[]{:S(2)}) collective-permute-start(bf16[3,8,8,512]{3,2,1,0:T(8,128)(2,1)S(1)} %pad_maximum_fusion.refs_2_), channel_id=1, source_target_pairs={{0,60},{4,0},{8,4},{12,8},{16,12},{20,16},{24,20},{28,24},{32,28},... | collective-permute-start | bytes 589832 | tf_op jit(solution)/shard_map/ppermute | solution.py:200
  73.9 10.5 %collective-permute-start.3 = (bf16[3,8,8,512]{3,2,1,0:T(8,128)(2,1)S(1)}, bf16[3,8,8,512]{3,2,1,0:T(8,128)(2,1)S(1)}, u32[]{:S(2)}, u32[]{:S(2)}) collective-permute-start(bf16[3,8,8,512]{3,2,1,0:T(8,128)(2,1)S(1)} %pad_maximum_fusion.refs_2_), channel_id=1, source_target_pairs={{0,4},{4,8},{8,12},{12,16},{16,20},{20,24},{24,28},{28,32},{32,36}... | collective-permute-start | bytes 589832 | tf_op jit(solution)/shard_map/ppermute | solution.py:200
  77.8 16.8 %collective-permute-start.6 = (bf16[4,8,512]{2,1,0:T(8,128)(2,1)S(1)}, bf16[4,8,512]{2,1,0:T(8,128)(2,1)S(1)}, u32[]{:S(2)}, u32[]{:S(2)}) collective-permute-start(bf16[4,8,512]{2,1,0:T(8,128)(2,1)S(1)} %slice_bitcast_fusion.1), channel_id=1, source_target_pairs={{0,56},{4,60},{8,0},{12,4},{16,8},{20,12},{24,16},{28,20},{32,24},... | collective-permute-start | bytes 98312 | tf_op jit(solution)/shard_map/ppermute | solution.py:200
  82.5 13.8 %collective-permute-start.4 = (bf16[3,8,8,512]{3,2,1,0:T(8,128)(2,1)S(1)}, bf16[3,8,8,512]{3,2,1,0:T(8,128)(2,1)S(1)}, u32[]{:S(2)}, u32[]{:S(2)}) collective-permute-start(bf16[3,8,8,512]{3,2,1,0:T(8,128)(2,1)S(1)} %collective-permute-done.2.refs_3_), channel_id=1, source_target_pairs={{0,60},{4,0},{8,4},{12,8},{16,12},{20,16},{24,20},{28,24},{32,28},... | collective-permute-start | bytes 589832 | tf_op jit(solution)/shard_map/ppermute | solution.py:200
  84.4 11.9 %collective-permute-start.5 = (bf16[3,8,8,512]{3,2,1,0:T(8,128)(2,1)S(1)}, bf16[3,8,8,512]{3,2,1,0:T(8,128)(2,1)S(1)}, u32[]{:S(2)}, u32[]{:S(2)}) collective-permute-start(bf16[3,8,8,512]{3,2,1,0:T(8,128)(2,1)S(1)} %collective-permute-done.3.refs_4_), channel_id=1, source_target_pairs={{0,4},{4,8},{8,12},{12,16},{16,20},{20,24},{24,28},{28,32},{32,36}... | collective-permute-start | bytes 589832 | tf_op jit(solution)/shard_map/ppermute | solution.py:200
  88.3 7.9 %collective-permute-start.7 = (bf16[4,8,512]{2,1,0:T(8,128)(2,1)S(1)}, bf16[4,8,512]{2,1,0:T(8,128)(2,1)S(1)}, u32[]{:S(2)}, u32[]{:S(2)}) collective-permute-start(bf16[4,8,512]{2,1,0:T(8,128)(2,1)S(1)} %slice_bitcast_fusion), channel_id=1, source_target_pairs={{0,8},{4,12},{8,16},{12,20},{16,24},{20,28},{24,32},{28,36},{32,40... | collective-permute-start | bytes 98312 | tf_op jit(solution)/shard_map/ppermute | solution.py:200
  96.3 14.4 %copy-start.2 = (bf16[16,4096]{1,0:T(8,128)(2,1)S(1)}, bf16[16,4096]{1,0:T(8,128)(2,1)}, u32[]{:S(2)}) copy-start(bf16[16,4096]{1,0:T(8,128)(2,1)} %win_ref.3) | copy-start | bytes 393220
  97.9 12.8 %copy-start = (bf16[172,4096]{1,0:T(8,128)(2,1)S(1)}, bf16[172,4096]{1,0:T(8,128)(2,1)}, u32[]{:S(2)}) copy-start(bf16[172,4096]{1,0:T(8,128)(2,1)} %weight_ref.1) | copy-start | bytes 4227076
  97.9 4.5 %collective-permute-start.9 = (f32[176,512]{1,0:T(8,128)S(1)}, f32[176,512]{1,0:T(8,128)S(1)}, u32[]{:S(2)}, u32[]{:S(2)}) collective-permute-start(f32[176,512]{1,0:T(8,128)S(1)} %get-tuple-element.13), channel_id=1, source_target_pairs={{0,1},{1,0},{2,3},{3,2},{4,5},{5,4},{6,7},{7,6},{8,9},{9,8},{10,11... | collective-permute-start | bytes 1081352 | tf_op jit(solution)/shard_map/ppermute | solution.py:204
  100.0 20.5 %collective-permute-start.8 = (f32[176,512]{1,0:T(8,128)S(1)}, f32[176,512]{1,0:T(8,128)}, u32[]{:S(2)}, u32[]{:S(2)}) collective-permute-start(f32[176,512]{1,0:T(8,128)S(1)} %get-tuple-element.11), channel_id=1, source_target_pairs={{0,1},{1,0},{2,3},{3,2},{4,5},{5,4},{6,7},{7,6},{8,9},{9,8},{10,11... | collective-permute-start | bytes 1081352 | tf_op jit(solution)/shard_map/ppermute | solution.py:204
  102.5 18.1 %collective-permute-start.10 = (f32[176,512]{1,0:T(8,128)S(1)}, f32[176,512]{1,0:T(8,128)}, u32[]{:S(2)}, u32[]{:S(2)}) collective-permute-start(f32[176,512]{1,0:T(8,128)S(1)} %add.10), channel_id=1, source_target_pairs={{0,2},{2,0},{1,3},{3,1},{4,6},{6,4},{5,7},{7,5},{8,10},{10,8},{9,1... | collective-permute-start | bytes 1081352 | tf_op jit(solution)/shard_map/ppermute | solution.py:204
  107.3 11.4 %all-to-all-start.1 = ((bf16[4,224,128]{2,1,0:T(8,128)(2,1)}), bf16[4,224,128]{2,1,0:T(8,128)(2,1)S(1)}, u32[]{:S(2)}, u32[]{:S(2)}) async-start(bf16[4,224,128]{2,1,0:T(8,128)(2,1)} %get-tuple-element.8), calls=%async_computation.1 | async-start | bytes 458752 | tf_op jit(solution)/shard_map/all_to_all | solution.py:208
where the time goes:
time: 123 us; the launch traced here: 122 us
  starting transfers between devices  72.3 us (59%)
  waiting for transfers between devices  35.3 us (29%)
  Pallas kernels  7.68 us (6%)
  local copies, waits for them, and re-layouts  4.17 us (3%)
  other arithmetic  2.07 us (2%)
    ppermute x8, starting transfers between devices, shifted(): return lax.ppermute(value, 'z', [(i, (i - offset) % n) for i in range(n)])  33.9 us
    all_to_all x4, starting transfers between devices, exchanged(): return lax.all_to_all(value, axis, 0, 0, tiled=True)  29.2 us
    all_to_all x4, waiting for transfers between devices, exchanged(): return lax.all_to_all(value, axis, 0, 0, tiled=True)  25.5 us
    ppermute x8, waiting for transfers between devices, shifted(): return lax.ppermute(value, 'z', [(i, (i - offset) % n) for i in range(n)])  9.85 us
    ppermute x3, starting transfers between devices, swapped(): return lax.ppermute(value, axis, [(0, 1), (1, 0)])  9.27 us
    pallas_call x6, Pallas kernels, call(): pl.pallas_call(body, out_shape=out_shape, in_specs=[scalar if i in smem e...  7.68 us
    unnamed x14, local copies, waits for them, and re-layouts  4.16 us
  transfers between devices with their start and end apart: 15, of which 7 were waited for; matrix products, arithmetic and copies ran while one was open for 0% of the time, Pallas kernels for 4%

commit v1 on v0

--- a/solution.py
+++ b/solution.py
@@ -38,7 +38,7 @@
         out_specs=[vmem] * len(out_shape) if many else vmem,
         scratch_shapes=list(scratch),
         cost_estimate=pl.CostEstimate(flops=flops, bytes_accessed=1 << 20, transcendentals=0),
-        compiler_params=pltpu.CompilerParams(vmem_limit_bytes=40 << 20),
+        compiler_params=pltpu.CompilerParams(vmem_limit_bytes=16 << 20),
     )(*args)
 
 
@@ -109,12 +109,14 @@
         out_ref[z] = jnp.concatenate(block, axis=1).astype(BF16)
 
 
-def turn_b(in_ref, w_ref, p_ref):
+def turn_b(in_ref, w_ref, *refs):
+    p_refs, hold_ref = refs[:-1], refs[-1]
     nz, rows, lanes = in_ref.shape
-    nq, tall, _ = p_ref.shape
+    nq = len(p_refs)
+    tall = p_refs[0].shape[0]
     hidden = w_ref.shape[1]
-    step = hidden // nq
-    proj = tall - step
+    block = hidden // nq
+    proj = tall - block
     x = in_ref[...].astype(F32).reshape(nz * rows, lanes).T
     at = hidden + proj
     fit = x[at : at + 1] + (x[at + 1 : at + 2] + x[at + 2 : at + 3])
@@ -122,11 +124,13 @@
     weighted = (b * fit).astype(BF16)
     for g in range(w_ref.shape[0]):
         w_ref[g] = weighted
-    b = b.astype(BF16)
+    hold_ref[...] = b.astype(BF16)
     extra = x[hidden:at].astype(BF16)
-    for q in range(nq):
-        p_ref[q, :step] = b[q * step : (q + 1) * step]
-        p_ref[q, step:] = extra
+    q = lax.axis_index("yhi") * 2 + lax.axis_index("core")
+    for j, ref in enumerate(p_refs):
+        start = pl.multiple_of((q ^ j) * block, 8)
+        ref[:block] = hold_ref[pl.ds(start, block), :]
+        ref[block:] = extra
 
 
 def base_rows(weight_ref, win_ref, out_ref):
@@ -135,14 +139,18 @@
     out_ref[...] = lax.dot_general(weight_ref[...], spread, NT, preferred_element_type=F32)
 
 
-def perturb(scale, in_ref, base_ref, out_ref):
-    nq, tall, lanes = in_ref.shape
+def perturb(scale, base_ref, *refs):
+    in_refs, out_ref, hold_ref = refs[:-2], refs[-2], refs[-1]
+    nq, tall, lanes = hold_ref.shape
+    own_q = lax.axis_index("yhi") * 2 + lax.axis_index("core")
+    for j, ref in enumerate(in_refs):
+        hold_ref[own_q ^ j] = ref[...]
     own = base_ref.shape[0]
     step = up8(own)
     tok = (tall - step) // PARTS
     rank = 4
     wide = nq * lanes
-    x = jnp.concatenate([in_ref[q] for q in range(nq)], axis=1)
+    x = jnp.concatenate([hold_ref[q] for q in range(nq)], axis=1)
     source = lax.broadcasted_iota(jnp.int32, (wide, wide), 0)
     target = lax.broadcasted_iota(jnp.int32, (wide, wide), 1)
     place = ((source & 127) >> 3) * 32 + (source >> 7) * 8 + (source & 7)
@@ -166,29 +174,22 @@
         out_ref[:, part * cands * tok : (part + 1) * cands * tok] = out.astype(BF16)
 
 
-OFFSETS = ((0, 5, -5), (1, 6, -4), (-1, 4, -6), (2, 7, -3), (-2, 3, -7))
+OFFSETS = ((0, 5, -5), (1, 6, -4), (-1, 4, -6), (2, 7, -3), (-2, 3, -7), (8,))
 
 
 def update_parts(*refs):
-    at_ref, w_ref = refs[:2]
-    chunks, (first_ref, second_ref) = refs[2:7], refs[7:9]
-    out_refs = refs[9:13]
-    rows_ref, sum_ref = refs[13:]
+    w_ref, chunks, out_refs = refs[0], refs[1:7], refs[7:11]
+    rows_ref, sum_ref = refs[11:]
     groups, nz, rows, width = rows_ref.shape
-    z = at_ref[0]
+    z, y, core = (lax.axis_index(name) for name in SHARD)
     for ref, offsets in zip(chunks, OFFSETS):
         for i, offset in enumerate(offsets):
             place = lax.rem(z + offset + nz, nz)
             for g in range(groups):
                 rows_ref[g, place] = ref[i, g]
-    place = lax.rem(z + nz // 2, nz)
-    for g in range(groups // 2):
-        rows_ref[g, place] = first_ref[g]
-        rows_ref[groups // 2 + g, place] = second_ref[g]
     left = jnp.concatenate([w_ref[g] for g in range(groups)], axis=1)
     right = rows_ref[...].reshape(groups * nz * rows, width)
     sum_ref[...] = jnp.dot(left, right, preferred_element_type=F32)
-    y, core = at_ref[1], at_ref[2]
     tall = out_refs[0].shape[0]
     for ref, yy, cc in zip(out_refs, (y, y, 1 - y, 1 - y), (core, 1 - core, core, 1 - core)):
         start = pl.multiple_of((yy * 2 + cc) * tall, 8)
@@ -202,6 +203,10 @@
 
 def swapped(value, axis):
     return lax.ppermute(value, axis, [(0, 1), (1, 0)])
+
+
+def turned(value, j):
+    return lax.ppermute(value, Q, [(q, q ^ j) for q in range(4)])
 
 
 def exchanged(value, axis):
@@ -233,44 +238,41 @@
         smem=(0,),
     )
     columns = exchanged(packed, "z")
-    weighted, pieces = call(
+    tall = block + PARTS * tok
+    weighted, *pieces = call(
         turn_b,
-        [
-            shape((groups, nq * block, nz * rows), BF16),
-            shape((nq, block + PARTS * tok, nz * rows), BF16),
-        ],
+        [shape((groups, nq * block, nz * rows), BF16)] + [shape((tall, nz * rows), BF16)] * nq,
         (columns,),
         1 << 24,
+        scratch=[pltpu.VMEM((nq * block, nz * rows), BF16)],
     )
     weighted = exchanged(weighted, "grp")
-    pieces = exchanged(pieces, Q)
+    pieces[1:] = [turned(pieces[j], j) for j in range(1, nq)]
     base = call(base_rows, shape((own, LANE), F32), (weight, window), 1 << 28)
     perturbed = call(
         functools.partial(perturb, 0.25 / math.sqrt(depth)),
         shape((own, cands * nz * nq * tok), BF16),
-        (pieces, base),
+        (base, *pieces),
         1 << 30,
+        scratch=[pltpu.VMEM((nq, tall, nz * rows), BF16)],
     )
 
     mine = mine[None]
-    near = jnp.concatenate([mine, shifted(mine, 5), shifted(mine, -5)], axis=0)
+    far = shifted(mine, 5)
+    near = jnp.concatenate([mine, far, shifted(mine, -5)], axis=0)
     up, down = shifted(near, 1), shifted(near, -1)
     up2, down2 = shifted(up, 1), shifted(down, -1)
-    half = groups // 2
-    first = shifted(up[1, :half], 2)
-    second = shifted(down[2, half:], -2)
-    at = jnp.stack([lax.axis_index("z"), lax.axis_index("yhi"), lax.axis_index("core")])
+    across = shifted(far, 3)
     part = shape((block, width), F32)
     oo, ox, xo, xx = call(
         update_parts,
         [part] * 4,
-        (at.astype(jnp.int32), weighted, near, up, down, up2, down2, first, second),
+        (weighted, near, up, down, up2, down2, across),
         1 << 30,
         scratch=[
             pltpu.VMEM((groups, nz, rows, width), BF16),
             pltpu.VMEM((nq * block, width), F32),
         ],
-        smem=(0,),
     )
     there = xo + swapped(xx, "core")
     here = oo + swapped(ox, "core")

time: 123 us -> 123 us (level)
  the two profiles are of different devices: /device:TPU:34 before, /device:TPU:99 now
where the time goes in v1:
time: 123 us; the launch traced here: 122 us
  starting transfers between devices  78.8 us (64%)
  waiting for transfers between devices  30.3 us (25%)
  Pallas kernels  7.17 us (6%)
  local copies, waits for them, and re-layouts  4.16 us (3%)
    ppermute x7, starting transfers between devices, shifted(): return lax.ppermute(value, 'z', [(i, (i - offset) % n) for i in range(n)])  26.3 us
    all_to_all x3, starting transfers between devices, exchanged(): return lax.all_to_all(value, axis, 0, 0, tiled=True)  23.5 us
    ppermute x3, starting transfers between devices, swapped(): return lax.ppermute(value, axis, [(0, 1), (1, 0)])  19.3 us
    all_to_all x3, waiting for transfers between devices, exchanged(): return lax.all_to_all(value, axis, 0, 0, tiled=True)  16.3 us
    ppermute x7, waiting for transfers between devices, shifted(): return lax.ppermute(value, 'z', [(i, (i - offset) % n) for i in range(n)])  12.1 us
    ppermute x3, starting transfers between devices, turned(): return lax.ppermute(value, Q, [(q, q ^ j) for q in range(4)])  9.65 us
    pallas_call x6, Pallas kernels, call(): pl.pallas_call(body, out_shape=out_shape, in_specs=[scalar if i in smem e...  7.17 us
    unnamed x14, local copies, waits for them, and re-layouts  4.16 us
  transfers between devices with their start and end apart: 16, of which 7 were waited for; matrix products, arithmetic and copies ran while one was open for 0% of the time, Pallas kernels for 4%

profile of v1, /device:TPU:99, one launch (start us, length us, event | category | flops | bytes accessed | tf_op | source)
XLA Modules:
  0.0 122.2 jit_solution(13847661429337103542)
XLA Ops:
  0.6 0.0 copy-start.1
  0.6 0.9 copy-done.1
  1.5 0.0 copy-start.3
  1.5 0.8 copy-done.3
  2.4 0.0 copy-start.5
  2.4 0.9 copy-done.5
  3.3 0.0 copy-start.6
  3.3 0.7 copy-done.6
  4.0 1.6 %shard_map.69 = bf16[16,8,768]{2,1,0:T(8,128)(2,1)} custom-call(f32[2]{0:T(128)S(1)} %copy-done.6, bf16[16,4096]{1,0:T(8,128)(2,1)S(1)} %copy-done.1, bf16[2,4,4096]{2,1,0:T(4,128)(2,1)S(1)} %copy-done.3, bf16[2,4,11008]{2,1,0:T(4,128)(2,1)S(1)} %copy-done.5), custom_call_target="tpu_custom_call" | custom-call | flops 16777216 | bytes 1048576 | tf_op jit(solution)/shard_map/pallas_call | solution.py:34
  5.6 13.7 %all-to-all-start = ((bf16[16,8,768]{2,1,0:T(8,128)(2,1)}), bf16[16,8,768]{2,1,0:T(8,128)(2,1)S(1)}, u32[]{:S(2)}, u32[]{:S(2)}) async-start(bf16[16,8,768]{2,1,0:T(8,128)(2,1)} %shard_map.69), calls=%async_computation | async-start | bytes 393216 | tf_op jit(solution)/shard_map/all_to_all | solution.py:213
  19.3 0.0 copy-start.4
  19.3 0.8 copy-done.4
  20.2 0.6 shard_map.72
  20.8 13.5 %all-to-all-done.in_ref = bf16[16,8,768]{2,1,0:T(8,128)(2,1)S(1)} async-done(((bf16[16,8,768]{2,1,0:T(8,128)(2,1)}), bf16[16,8,768]{2,1,0:T(8,128)(2,1)S(1)}, u32[]{:S(2)}, u32[]{:S(2)}) %all-to-all-start) | async-done | bytes 196640 | tf_op jit(solution)/shard_map/all_to_all | solution.py:213
  34.3 5.3 %all-to-all-start.2 = ((bf16[8,8,512]{2,1,0:T(8,128)(2,1)}), bf16[8,8,512]{2,1,0:T(8,128)(2,1)S(1)}, u32[]{:S(2)}, u32[]{:S(2)}) async-start(bf16[8,8,512]{2,1,0:T(8,128)(2,1)} %shard_map.72), calls=%async_computation.2 | async-start | bytes 131072 | tf_op jit(solution)/shard_map/all_to_all | solution.py:213
  39.6 1.4 %shard_map.70 = (bf16[8,704,128]{2,1,0:T(8,128)(2,1)}, bf16[224,128]{1,0:T(8,128)(2,1)S(1)}, bf16[224,128]{1,0:T(8,128)(2,1)S(1)}, bf16[224,128]{1,0:T(8,128)(2,1)S(1)}, bf16[224,128]{1,0:T(8,128)(2,1)S(1)}) custom-call(bf16[16,8,768]{2,1,0:T(8,128)(2,1)S(1)} %all-to-all-done.in_ref), custom_call_target="tpu_custom_call" | custom-call | flops 16777216 | bytes 1048576 | tf_op jit(solution)/shard_map/pallas_call | solution.py:34
  41.0 2.8 %all-to-all-done.2 = bf16[8,8,512]{2,1,0:T(8,128)(2,1)S(1)} async-done(((bf16[8,8,512]{2,1,0:T(8,128)(2,1)}), bf16[8,8,512]{2,1,0:T(8,128)(2,1)S(1)}, u32[]{:S(2)}, u32[]{:S(2)}) %all-to-all-start.2) | async-done | bytes 65568 | tf_op jit(solution)/shard_map/all_to_all | solution.py:213
  43.8 4.5 %all-to-all-start.1 = ((bf16[8,704,128]{2,1,0:T(8,128)(2,1)}), bf16[8,704,128]{2,1,0:T(8,128)(2,1)S(1)}, u32[]{:S(2)}, u32[]{:S(2)}) async-start(bf16[8,704,128]{2,1,0:T(8,128)(2,1)} %get-tuple-element.15), calls=%async_computation.1 | async-start | bytes 2883584 | tf_op jit(solution)/shard_map/all_to_all | solution.py:213
  48.3 3.5 %collective-permute-start.3 = (bf16[1,8,8,512]{3,2,1,0:T(8,128)(2,1)S(1)}, bf16[1,8,8,512]{3,2,1,0:T(8,128)(2,1)S(1)}, u32[]{:S(2)}, u32[]{:S(2)}) collective-permute-start(bf16[1,8,8,512]{3,2,1,0:T(8,128)(2,1)S(1)} %bitcast.1), channel_id=1, source_target_pairs={{0,44},{4,48},{8,52},{12,56},{16,60},{20,0},{24,4},{28,8},{32,12},... | collective-permute-start | bytes 196616 | tf_op jit(solution)/shard_map/ppermute | solution.py:201
  51.8 7.8 %collective-permute-start.4 = (bf16[1,8,8,512]{3,2,1,0:T(8,128)(2,1)S(1)}, bf16[1,8,8,512]{3,2,1,0:T(8,128)(2,1)S(1)}, u32[]{:S(2)}, u32[]{:S(2)}) collective-permute-start(bf16[1,8,8,512]{3,2,1,0:T(8,128)(2,1)S(1)} %bitcast.2), channel_id=1, source_target_pairs={{0,20},{4,24},{8,28},{12,32},{16,36},{20,40},{24,44},{28,48},{32,5... | collective-permute-start | bytes 196616 | tf_op jit(solution)/shard_map/ppermute | solution.py:201
  59.6 0.3 collective-permute-done.3
  59.9 3.4 %collective-permute-done.4 = bf16[1,8,8,512]{3,2,1,0:T(8,128)(2,1)S(1)} collective-permute-done((bf16[1,8,8,512]{3,2,1,0:T(8,128)(2,1)S(1)}, bf16[1,8,8,512]{3,2,1,0:T(8,128)(2,1)S(1)}, u32[]{:S(2)}, u32[]{:S(2)}) %collective-permute-start.4) | collective-permute-done | bytes 65568 | tf_op jit(solution)/shard_map/ppermute | solution.py:201
  63.3 0.0 copy-start.2
  63.3 3.7 %collective-permute-start.5 = (bf16[3,8,8,512]{3,2,1,0:T(8,128)(2,1)S(1)}, bf16[3,8,8,512]{3,2,1,0:T(8,128)(2,1)S(1)}, u32[]{:S(2)}, u32[]{:S(2)}) collective-permute-start(bf16[3,8,8,512]{3,2,1,0:T(8,128)(2,1)S(1)} %pad_maximum_fusion.refs_1_), channel_id=1, source_target_pairs={{0,60},{4,0},{8,4},{12,8},{16,12},{20,16},{24,20},{28,24},{32,28},... | collective-permute-start | bytes 589832 | tf_op jit(solution)/shard_map/ppermute | solution.py:201
  67.0 2.9 %collective-permute-start.6 = (bf16[3,8,8,512]{3,2,1,0:T(8,128)(2,1)S(1)}, bf16[3,8,8,512]{3,2,1,0:T(8,128)(2,1)S(1)}, u32[]{:S(2)}, u32[]{:S(2)}) collective-permute-start(bf16[3,8,8,512]{3,2,1,0:T(8,128)(2,1)S(1)} %pad_maximum_fusion.refs_1_), channel_id=1, source_target_pairs={{0,4},{4,8},{8,12},{12,16},{16,20},{20,24},{24,28},{28,32},{32,36}... | collective-permute-start | bytes 589832 | tf_op jit(solution)/shard_map/ppermute | solution.py:201
  69.9 1.1 collective-permute-done.5.refs_2_
  71.1 2.4 %collective-permute-start.7 = (bf16[3,8,8,512]{3,2,1,0:T(8,128)(2,1)S(1)}, bf16[3,8,8,512]{3,2,1,0:T(8,128)(2,1)S(1)}, u32[]{:S(2)}, u32[]{:S(2)}) collective-permute-start(bf16[3,8,8,512]{3,2,1,0:T(8,128)(2,1)S(1)} %collective-permute-done.5.refs_2_), channel_id=1, source_target_pairs={{0,60},{4,0},{8,4},{12,8},{16,12},{20,16},{24,20},{28,24},{32,28},... | collective-permute-start | bytes 589832 | tf_op jit(solution)/shard_map/ppermute | solution.py:201
  73.4 0.0 collective-permute-done.6.refs_3_
  73.5 4.1 %collective-permute-start.8 = (bf16[3,8,8,512]{3,2,1,0:T(8,128)(2,1)S(1)}, bf16[3,8,8,512]{3,2,1,0:T(8,128)(2,1)S(1)}, u32[]{:S(2)}, u32[]{:S(2)}) collective-permute-start(bf16[3,8,8,512]{3,2,1,0:T(8,128)(2,1)S(1)} %collective-permute-done.6.refs_3_), channel_id=1, source_target_pairs={{0,4},{4,8},{8,12},{12,16},{16,20},{20,24},{24,28},{28,32},{32,36}... | collective-permute-start | bytes 589832 | tf_op jit(solution)/shard_map/ppermute | solution.py:201
  77.6 1.9 %collective-permute-start.9 = (bf16[1,8,8,512]{3,2,1,0:T(8,128)(2,1)S(1)}, bf16[1,8,8,512]{3,2,1,0:T(8,128)(2,1)S(1)}, u32[]{:S(2)}, u32[]{:S(2)}) collective-permute-start(bf16[1,8,8,512]{3,2,1,0:T(8,128)(2,1)S(1)} %collective-permute-done.3), channel_id=1, source_target_pairs={{0,52},{4,56},{8,60},{12,0},{16,4},{20,8},{24,12},{28,16},{32,20},... | collective-permute-start | bytes 196616 | tf_op jit(solution)/shard_map/ppermute | solution.py:201
  79.5 7.3 %collective-permute-done.9.refs_6_ = bf16[1,8,8,512]{3,2,1,0:T(8,128)(2,1)S(1)} collective-permute-done((bf16[1,8,8,512]{3,2,1,0:T(8,128)(2,1)S(1)}, bf16[1,8,8,512]{3,2,1,0:T(8,128)(2,1)S(1)}, u32[]{:S(2)}, u32[]{:S(2)}) %collective-permute-start.9) | collective-permute-done | bytes 65568 | tf_op jit(solution)/shard_map/ppermute | solution.py:201
  86.8 0.0 collective-permute-done.7.refs_4_
  86.8 0.0 collective-permute-done.8.refs_5_
  86.8 0.0 all-to-all-done.1.refs_0_
  86.8 0.0 copy-start
  86.8 1.1 shard_map.73
  87.9 12.9 %collective-permute-start.11 = (f32[176,512]{1,0:T(8,128)S(1)}, f32[176,512]{1,0:T(8,128)S(1)}, u32[]{:S(2)}, u32[]{:S(2)}) collective-permute-start(f32[176,512]{1,0:T(8,128)S(1)} %get-tuple-element.19), channel_id=1, source_target_pairs={{0,1},{1,0},{2,3},{3,2},{4,5},{5,4},{6,7},{7,6},{8,9},{9,8},{10,11... | collective-permute-start | bytes 1081352 | tf_op jit(solution)/shard_map/ppermute | solution.py:205
  100.8 1.9 %collective-permute-start.10 = (f32[176,512]{1,0:T(8,128)S(1)}, f32[176,512]{1,0:T(8,128)S(1)}, u32[]{:S(2)}, u32[]{:S(2)}) collective-permute-start(f32[176,512]{1,0:T(8,128)S(1)} %get-tuple-element.17), channel_id=1, source_target_pairs={{0,1},{1,0},{2,3},{3,2},{4,5},{5,4},{6,7},{7,6},{8,9},{9,8},{10,11... | collective-permute-start | bytes 1081352 | tf_op jit(solution)/shard_map/ppermute | solution.py:205
  102.7 0.0 collective-permute-done.11
  102.7 0.1 add.10
  102.8 4.5 %collective-permute-start.12 = (f32[176,512]{1,0:T(8,128)S(1)}, f32[176,512]{1,0:T(8,128)S(1)}, u32[]{:S(2)}, u32[]{:S(2)}) collective-permute-start(f32[176,512]{1,0:T(8,128)S(1)} %add.10), channel_id=1, source_target_pairs={{0,2},{2,0},{1,3},{3,1},{4,6},{6,4},{5,7},{7,5},{8,10},{10,8},{9,1... | collective-permute-start | bytes 1081352 | tf_op jit(solution)/shard_map/ppermute | solution.py:205
  107.3 2.7 %collective-permute-start = (bf16[224,128]{1,0:T(8,128)(2,1)S(1)}, bf16[224,128]{1,0:T(8,128)(2,1)S(1)}, u32[]{:S(2)}, u32[]{:S(2)}) collective-permute-start(bf16[224,128]{1,0:T(8,128)(2,1)S(1)} %get-tuple-element.12), channel_id=1, source_target_pairs={{0,1},{1,0},{2,3},{3,2},{4,5},{5,4},{6,7},{7,6},{8,9},{9,8},{10,11... | collective-permute-start | bytes 172040 | tf_op jit(solution)/shard_map/ppermute | solution.py:209
  110.0 2.3 %collective-permute-start.1 = (bf16[224,128]{1,0:T(8,128)(2,1)S(1)}, bf16[224,128]{1,0:T(8,128)(2,1)S(1)}, u32[]{:S(2)}, u32[]{:S(2)}) collective-permute-start(bf16[224,128]{1,0:T(8,128)(2,1)S(1)} %get-tuple-element.13), channel_id=1, source_target_pairs={{0,2},{1,3},{2,0},{3,1},{4,6},{5,7},{6,4},{7,5},{8,10},{9,11},{10,... | collective-permute-start | bytes 172040 | tf_op jit(solution)/shard_map/ppermute | solution.py:209
  112.3 4.7 %collective-permute-start.2 = (bf16[224,128]{1,0:T(8,128)(2,1)S(1)}, bf16[224,128]{1,0:T(8,128)(2,1)S(1)}, u32[]{:S(2)}, u32[]{:S(2)}) collective-permute-start(bf16[224,128]{1,0:T(8,128)(2,1)S(1)} %get-tuple-element.14), channel_id=1, source_target_pairs={{0,3},{1,2},{2,1},{3,0},{4,7},{5,6},{6,5},{7,4},{8,11},{9,10},{10,... | collective-permute-start | bytes 172040 | tf_op jit(solution)/shard_map/ppermute | solution.py:209
  117.0 0.0 copy-done.2
  117.0 0.0 copy-done
  117.0 0.5 shard_map.68.base_ref
  117.5 0.0 collective-permute-done.refs_1_
  117.6 0.0 collective-permute-done.1.refs_2_
  117.6 1.9 %collective-permute-done.2.refs_3_ = bf16[224,128]{1,0:T(8,128)(2,1)S(1)} collective-permute-done((bf16[224,128]{1,0:T(8,128)(2,1)S(1)}, bf16[224,128]{1,0:T(8,128)(2,1)S(1)}, u32[]{:S(2)}, u32[]{:S(2)}) %collective-permute-start.2) | collective-permute-done | bytes 57376 | tf_op jit(solution)/shard_map/ppermute | solution.py:209
  119.5 1.9 %shard_map.71 = bf16[172,2048]{1,0:T(8,128)(2,1)} custom-call(f32[172,128]{1,0:T(8,128)S(1)} %shard_map.68.base_ref, bf16[224,128]{1,0:T(8,128)(2,1)S(1)} %get-tuple-element.11.refs_0_, bf16[224,128]{1,0:T(8,128)(2,1)S(1)} %collective-permute-done.refs_1_, bf16[224,128]{1,0:T(8,128)(2,1)S(1)} %collective-permute-done.1.refs_2_, ...), custom_call_target="tpu_custom_call" | custom-call | flops 1073741824 | bytes 1048576 | tf_op jit(solution)/shard_map/pallas_call | solution.py:34
  121.3 0.0 collective-permute-done.10
  121.3 0.0 collective-permute-done.12
  121.3 0.8 fusion
  (1 shorter events, 0.0 us)
Async XLA Ops:
  0.6 0.9 copy-start.1
  1.5 0.8 copy-start.3
  2.4 0.9 copy-start.5
  3.3 0.7 copy-start.6
  5.6 28.7 %all-to-all-start = ((bf16[16,8,768]{2,1,0:T(8,128)(2,1)}), bf16[16,8,768]{2,1,0:T(8,128)(2,1)S(1)}, u32[]{:S(2)}, u32[]{:S(2)}) async-start(bf16[16,8,768]{2,1,0:T(8,128)(2,1)} %shard_map.69), calls=%async_computation | async-start | bytes 393216 | tf_op jit(solution)/shard_map/all_to_all | solution.py:213
  19.3 0.8 copy-start.4
  34.3 9.5 %all-to-all-start.2 = ((bf16[8,8,512]{2,1,0:T(8,128)(2,1)}), bf16[8,8,512]{2,1,0:T(8,128)(2,1)S(1)}, u32[]{:S(2)}, u32[]{:S(2)}) async-start(bf16[8,8,512]{2,1,0:T(8,128)(2,1)} %shard_map.72), calls=%async_computation.2 | async-start | bytes 131072 | tf_op jit(solution)/shard_map/all_to_all | solution.py:213
  43.8 43.0 %all-to-all-start.1 = ((bf16[8,704,128]{2,1,0:T(8,128)(2,1)}), bf16[8,704,128]{2,1,0:T(8,128)(2,1)S(1)}, u32[]{:S(2)}, u32[]{:S(2)}) async-start(bf16[8,704,128]{2,1,0:T(8,128)(2,1)} %get-tuple-element.15), calls=%async_computation.1 | async-start | bytes 2883584 | tf_op jit(solution)/shard_map/all_to_all | solution.py:213
  48.3 11.6 %collective-permute-start.3 = (bf16[1,8,8,512]{3,2,1,0:T(8,128)(2,1)S(1)}, bf16[1,8,8,512]{3,2,1,0:T(8,128)(2,1)S(1)}, u32[]{:S(2)}, u32[]{:S(2)}) collective-permute-start(bf16[1,8,8,512]{3,2,1,0:T(8,128)(2,1)S(1)} %bitcast.1), channel_id=1, source_target_pairs={{0,44},{4,48},{8,52},{12,56},{16,60},{20,0},{24,4},{28,8},{32,12},... | collective-permute-start | bytes 196616 | tf_op jit(solution)/shard_map/ppermute | solution.py:201
  51.8 11.5 %collective-permute-start.4 = (bf16[1,8,8,512]{3,2,1,0:T(8,128)(2,1)S(1)}, bf16[1,8,8,512]{3,2,1,0:T(8,128)(2,1)S(1)}, u32[]{:S(2)}, u32[]{:S(2)}) collective-permute-start(bf16[1,8,8,512]{3,2,1,0:T(8,128)(2,1)S(1)} %bitcast.2), channel_id=1, source_target_pairs={{0,20},{4,24},{8,28},{12,32},{16,36},{20,40},{24,44},{28,48},{32,5... | collective-permute-start | bytes 196616 | tf_op jit(solution)/shard_map/ppermute | solution.py:201
  63.3 53.7 %copy-start.2 = (bf16[16,4096]{1,0:T(8,128)(2,1)S(1)}, bf16[16,4096]{1,0:T(8,128)(2,1)}, u32[]{:S(2)}) copy-start(bf16[16,4096]{1,0:T(8,128)(2,1)} %win_ref.3) | copy-start | bytes 393220
  63.3 7.8 %collective-permute-start.5 = (bf16[3,8,8,512]{3,2,1,0:T(8,128)(2,1)S(1)}, bf16[3,8,8,512]{3,2,1,0:T(8,128)(2,1)S(1)}, u32[]{:S(2)}, u32[]{:S(2)}) collective-permute-start(bf16[3,8,8,512]{3,2,1,0:T(8,128)(2,1)S(1)} %pad_maximum_fusion.refs_1_), channel_id=1, source_target_pairs={{0,60},{4,0},{8,4},{12,8},{16,12},{20,16},{24,20},{28,24},{32,28},... | collective-permute-start | bytes 589832 | tf_op jit(solution)/shard_map/ppermute | solution.py:201
  67.0 6.4 %collective-permute-start.6 = (bf16[3,8,8,512]{3,2,1,0:T(8,128)(2,1)S(1)}, bf16[3,8,8,512]{3,2,1,0:T(8,128)(2,1)S(1)}, u32[]{:S(2)}, u32[]{:S(2)}) collective-permute-start(bf16[3,8,8,512]{3,2,1,0:T(8,128)(2,1)S(1)} %pad_maximum_fusion.refs_1_), channel_id=1, source_target_pairs={{0,4},{4,8},{8,12},{12,16},{16,20},{20,24},{24,28},{28,32},{32,36}... | collective-permute-start | bytes 589832 | tf_op jit(solution)/shard_map/ppermute | solution.py:201
  71.1 15.7 %collective-permute-start.7 = (bf16[3,8,8,512]{3,2,1,0:T(8,128)(2,1)S(1)}, bf16[3,8,8,512]{3,2,1,0:T(8,128)(2,1)S(1)}, u32[]{:S(2)}, u32[]{:S(2)}) collective-permute-start(bf16[3,8,8,512]{3,2,1,0:T(8,128)(2,1)S(1)} %collective-permute-done.5.refs_2_), channel_id=1, source_target_pairs={{0,60},{4,0},{8,4},{12,8},{16,12},{20,16},{24,20},{28,24},{32,28},... | collective-permute-start | bytes 589832 | tf_op jit(solution)/shard_map/ppermute | solution.py:201
  73.5 13.3 %collective-permute-start.8 = (bf16[3,8,8,512]{3,2,1,0:T(8,128)(2,1)S(1)}, bf16[3,8,8,512]{3,2,1,0:T(8,128)(2,1)S(1)}, u32[]{:S(2)}, u32[]{:S(2)}) collective-permute-start(bf16[3,8,8,512]{3,2,1,0:T(8,128)(2,1)S(1)} %collective-permute-done.6.refs_3_), channel_id=1, source_target_pairs={{0,4},{4,8},{8,12},{12,16},{16,20},{20,24},{24,28},{28,32},{32,36}... | collective-permute-start | bytes 589832 | tf_op jit(solution)/shard_map/ppermute | solution.py:201
  77.6 9.2 %collective-permute-start.9 = (bf16[1,8,8,512]{3,2,1,0:T(8,128)(2,1)S(1)}, bf16[1,8,8,512]{3,2,1,0:T(8,128)(2,1)S(1)}, u32[]{:S(2)}, u32[]{:S(2)}) collective-permute-start(bf16[1,8,8,512]{3,2,1,0:T(8,128)(2,1)S(1)} %collective-permute-done.3), channel_id=1, source_target_pairs={{0,52},{4,56},{8,60},{12,0},{16,4},{20,8},{24,12},{28,16},{32,20},... | collective-permute-start | bytes 196616 | tf_op jit(solution)/shard_map/ppermute | solution.py:201
  86.8 30.2 %copy-start = (bf16[172,4096]{1,0:T(8,128)(2,1)S(1)}, bf16[172,4096]{1,0:T(8,128)(2,1)}, u32[]{:S(2)}) copy-start(bf16[172,4096]{1,0:T(8,128)(2,1)} %weight_ref.1) | copy-start | bytes 4227076
  87.9 14.8 %collective-permute-start.11 = (f32[176,512]{1,0:T(8,128)S(1)}, f32[176,512]{1,0:T(8,128)S(1)}, u32[]{:S(2)}, u32[]{:S(2)}) collective-permute-start(f32[176,512]{1,0:T(8,128)S(1)} %get-tuple-element.19), channel_id=1, source_target_pairs={{0,1},{1,0},{2,3},{3,2},{4,5},{5,4},{6,7},{7,6},{8,9},{9,8},{10,11... | collective-permute-start | bytes 1081352 | tf_op jit(solution)/shard_map/ppermute | solution.py:205
  100.8 20.6 %collective-permute-start.10 = (f32[176,512]{1,0:T(8,128)S(1)}, f32[176,512]{1,0:T(8,128)S(1)}, u32[]{:S(2)}, u32[]{:S(2)}) collective-permute-start(f32[176,512]{1,0:T(8,128)S(1)} %get-tuple-element.17), channel_id=1, source_target_pairs={{0,1},{1,0},{2,3},{3,2},{4,5},{5,4},{6,7},{7,6},{8,9},{9,8},{10,11... | collective-permute-start | bytes 1081352 | tf_op jit(solution)/shard_map/ppermute | solution.py:205
  102.8 18.6 %collective-permute-start.12 = (f32[176,512]{1,0:T(8,128)S(1)}, f32[176,512]{1,0:T(8,128)S(1)}, u32[]{:S(2)}, u32[]{:S(2)}) collective-permute-start(f32[176,512]{1,0:T(8,128)S(1)} %add.10), channel_id=1, source_target_pairs={{0,2},{2,0},{1,3},{3,1},{4,6},{6,4},{5,7},{7,5},{8,10},{10,8},{9,1... | collective-permute-start | bytes 1081352 | tf_op jit(solution)/shard_map/ppermute | solution.py:205
  107.3 10.2 %collective-permute-start = (bf16[224,128]{1,0:T(8,128)(2,1)S(1)}, bf16[224,128]{1,0:T(8,128)(2,1)S(1)}, u32[]{:S(2)}, u32[]{:S(2)}) collective-permute-start(bf16[224,128]{1,0:T(8,128)(2,1)S(1)} %get-tuple-element.12), channel_id=1, source_target_pairs={{0,1},{1,0},{2,3},{3,2},{4,5},{5,4},{6,7},{7,6},{8,9},{9,8},{10,11... | collective-permute-start | bytes 172040 | tf_op jit(solution)/shard_map/ppermute | solution.py:209
  110.0 7.6 %collective-permute-start.1 = (bf16[224,128]{1,0:T(8,128)(2,1)S(1)}, bf16[224,128]{1,0:T(8,128)(2,1)S(1)}, u32[]{:S(2)}, u32[]{:S(2)}) collective-permute-start(bf16[224,128]{1,0:T(8,128)(2,1)S(1)} %get-tuple-element.13), channel_id=1, source_target_pairs={{0,2},{1,3},{2,0},{3,1},{4,6},{5,7},{6,4},{7,5},{8,10},{9,11},{10,... | collective-permute-start | bytes 172040 | tf_op jit(solution)/shard_map/ppermute | solution.py:209
  112.3 7.2 %collective-permute-start.2 = (bf16[224,128]{1,0:T(8,128)(2,1)S(1)}, bf16[224,128]{1,0:T(8,128)(2,1)S(1)}, u32[]{:S(2)}, u32[]{:S(2)}) collective-permute-start(bf16[224,128]{1,0:T(8,128)(2,1)S(1)} %get-tuple-element.14), channel_id=1, source_target_pairs={{0,3},{1,2},{2,1},{3,0},{4,7},{5,6},{6,5},{7,4},{8,11},{9,10},{10,... | collective-permute-start | bytes 172040 | tf_op jit(solution)/shard_map/ppermute | solution.py:209

commit v2 on v1

--- a/solution.py
+++ b/solution.py
@@ -11,11 +11,10 @@
 
 
 F32, BF16 = jnp.float32, jnp.bfloat16
-Q = ("yhi", "core")
 SHARD = ("z", "yhi", "core")
 GRP_SHARD = ("grp", "z", "yhi", "core")
 LANE = 128
-PARTS = 3
+PARTS = 2
 NT = (((1,), (1,)), ((), ()))
 
 
@@ -58,18 +57,23 @@
         out_ref[g] = jnp.concatenate(both, axis=0).astype(BF16)
 
 
+def layout(own, tok):
+    first = up8(own)
+    second = first + PARTS * tok
+    return first, second, second + own, upl(second + own + 3)
+
+
 def pack_b(fit_ref, win_ref, a_ref, b_ref, out_ref, wide_ref):
-    nz, rows, lanes = out_ref.shape
+    blocks, rows, lanes = out_ref.shape
     cands, rank, hidden = b_ref.shape
     tok, depth = win_ref.shape
-    nq = 4
-    own = hidden // (nz * nq)
-    step = up8(own)
+    own = hidden // (2 * blocks)
+    proj_at, second, fit_at, _ = layout(own, tok)
     for c in range(cands):
         wide_ref[c * rank : (c + 1) * rank, :hidden] = b_ref[c].astype(F32)
     wide_ref[:, hidden:] = jnp.zeros((rows, wide_ref.shape[1] - hidden), F32)
     a_rows = jnp.concatenate([a_ref[c].astype(F32) for c in range(cands)], axis=0).astype(BF16)
-    first = nq * step % LANE
+    first = proj_at % LANE
     win = win_ref[...]
     spread = jnp.concatenate(
         [jnp.zeros((first, depth), BF16)]
@@ -80,57 +84,61 @@
     proj = lax.dot_general(a_rows, spread, NT, preferred_element_type=F32)
     lane = lax.broadcasted_iota(jnp.int32, (rows, LANE), 1)
     row = lax.broadcasted_iota(jnp.int32, (rows, LANE), 0)
-    hi, mid, lo = split3(proj)
-    extra = jnp.where(lane < first + tok, hi, jnp.where(lane < first + 2 * tok, mid, lo))
+    high, mid, _ = split3(proj)
+    extra = jnp.where(lane < first + tok, high, mid)
+    has_extra = (lane >= first) & (lane < first + PARTS * tok)
     fit = jnp.where(row < rank, fit_ref[0], fit_ref[1])
-    fhi, fmid, flo = split3(fit)
-    at = first + PARTS * tok
-    fits = jnp.where(lane == at, fhi, jnp.where(lane == at + 1, fmid, flo))
-    extra = jnp.where(lane < at, extra, jnp.where(lane < at + 3, fits, 0.0))
-    for z in range(nz):
-        block = [jnp.zeros((rows, LANE), F32) for _ in range(lanes // LANE)]
-        for q in range(nq):
-            source = (z * nq + q) * own
-            base = source // LANE * LANE
-            target = q * step
-            start = target // LANE
-            offset = target % LANE
-            span = min(3, len(block) - start)
-            window = wide_ref[:, base : base + 3 * LANE]
-            turn = (offset - (source - base)) % (3 * LANE)
-            if turn:
-                window = pltpu.roll(window, turn, 1)
-            for k in range(span):
-                at_lane = lane + k * LANE
-                inside = (at_lane >= offset) & (at_lane < offset + own)
-                piece = window[:, k * LANE : (k + 1) * LANE]
-                block[start + k] = jnp.where(inside, piece, block[start + k])
-        block[-1] = jnp.where(lane >= first, extra, block[-1])
-        out_ref[z] = jnp.concatenate(block, axis=1).astype(BF16)
-
-
-def turn_b(in_ref, w_ref, *refs):
-    p_refs, hold_ref = refs[:-1], refs[-1]
-    nz, rows, lanes = in_ref.shape
-    nq = len(p_refs)
-    tall = p_refs[0].shape[0]
-    hidden = w_ref.shape[1]
-    block = hidden // nq
-    proj = tall - block
-    x = in_ref[...].astype(F32).reshape(nz * rows, lanes).T
-    at = hidden + proj
-    fit = x[at : at + 1] + (x[at + 1 : at + 2] + x[at + 2 : at + 3])
-    b = x[:hidden]
-    weighted = (b * fit).astype(BF16)
-    for g in range(w_ref.shape[0]):
-        w_ref[g] = weighted
-    hold_ref[...] = b.astype(BF16)
-    extra = x[hidden:at].astype(BF16)
-    q = lax.axis_index("yhi") * 2 + lax.axis_index("core")
-    for j, ref in enumerate(p_refs):
-        start = pl.multiple_of((q ^ j) * block, 8)
-        ref[:block] = hold_ref[pl.ds(start, block), :]
-        ref[block:] = extra
+    fits = split3(fit)
+    at = fit_at % LANE
+    for z in range(blocks // 2):
+        for core in range(2):
+            block = [jnp.zeros((rows, LANE), F32) for _ in range(lanes // LANE)]
+            for y in range(2):
+                source = ((z * 2 + y) * 2 + core) * own
+                base = source // LANE * LANE
+                target = y * second
+                start = target // LANE
+                offset = target % LANE
+                span = min(3, len(block) - start)
+                window = wide_ref[:, base : base + 3 * LANE]
+                turn = (offset - (source - base)) % (3 * LANE)
+                if turn:
+                    window = pltpu.roll(window, turn, 1)
+                for k in range(span):
+                    at_lane = lane + k * LANE
+                    inside = (at_lane >= offset) & (at_lane < offset + own)
+                    piece = window[:, k * LANE : (k + 1) * LANE]
+                    block[start + k] = jnp.where(inside, piece, block[start + k])
+            place = proj_at // LANE
+            block[place] = jnp.where(has_extra, extra, block[place])
+            place = fit_at // LANE
+            for i, value in enumerate(fits):
+                block[place] = jnp.where(lane == at + i, value, block[place])
+            out_ref[z * 2 + core] = jnp.concatenate(block, axis=1).astype(BF16)
+
+
+def turn_b(own, tok, in_ref, w_ref, keep_ref, send_ref, hold_ref):
+    blocks, rows, lanes = in_ref.shape
+    proj_at, second, fit_at, _ = layout(own, tok)
+    block = proj_at
+    wide = blocks * rows // 2
+    x = in_ref[...].astype(F32).reshape(blocks // 2, 2, rows, lanes)
+    for core in range(2):
+        part = x[:, core].reshape(wide, lanes).T
+        fit = part[fit_at : fit_at + 1] + (
+            part[fit_at + 1 : fit_at + 2] + part[fit_at + 2 : fit_at + 3]
+        )
+        for y in range(2):
+            b = part[y * second : y * second + block]
+            weighted = (b * fit).astype(BF16)
+            for g in range(w_ref.shape[0] // 2):
+                w_ref[2 * g + core, y * block : (y + 1) * block] = weighted
+            across = slice(core * wide, (core + 1) * wide)
+            hold_ref[y, :block, across] = b.astype(BF16)
+            hold_ref[y, block:, across] = part[proj_at:second].astype(BF16)
+    y = lax.axis_index("yhi")
+    keep_ref[...] = hold_ref[y]
+    send_ref[...] = hold_ref[1 - y]
 
 
 def base_rows(weight_ref, win_ref, out_ref):
@@ -139,18 +147,17 @@
     out_ref[...] = lax.dot_general(weight_ref[...], spread, NT, preferred_element_type=F32)
 
 
-def perturb(scale, base_ref, *refs):
-    in_refs, out_ref, hold_ref = refs[:-2], refs[-2], refs[-1]
-    nq, tall, lanes = hold_ref.shape
-    own_q = lax.axis_index("yhi") * 2 + lax.axis_index("core")
-    for j, ref in enumerate(in_refs):
-        hold_ref[own_q ^ j] = ref[...]
+def perturb(scale, base_ref, keep_ref, got_ref, out_ref, hold_ref):
+    tall = keep_ref.shape[0]
+    own_y = lax.axis_index("yhi")
+    hold_ref[own_y] = keep_ref[...]
+    hold_ref[1 - own_y] = got_ref[...]
     own = base_ref.shape[0]
     step = up8(own)
     tok = (tall - step) // PARTS
     rank = 4
-    wide = nq * lanes
-    x = jnp.concatenate([hold_ref[q] for q in range(nq)], axis=1)
+    x = jnp.concatenate([hold_ref[0], hold_ref[1]], axis=1)
+    wide = x.shape[1]
     source = lax.broadcasted_iota(jnp.int32, (wide, wide), 0)
     target = lax.broadcasted_iota(jnp.int32, (wide, wide), 1)
     place = ((source & 127) >> 3) * 32 + (source >> 7) * 8 + (source & 7)
@@ -187,12 +194,14 @@
             place = lax.rem(z + offset + nz, nz)
             for g in range(groups):
                 rows_ref[g, place] = ref[i, g]
-    left = jnp.concatenate([w_ref[g] for g in range(groups)], axis=1)
+    left = jnp.concatenate(
+        [jnp.concatenate([w_ref[2 * g + c] for g in range(groups)], axis=1) for c in range(2)], axis=0
+    )
     right = rows_ref[...].reshape(groups * nz * rows, width)
     sum_ref[...] = jnp.dot(left, right, preferred_element_type=F32)
     tall = out_refs[0].shape[0]
     for ref, yy, cc in zip(out_refs, (y, y, 1 - y, 1 - y), (core, 1 - core, core, 1 - core)):
-        start = pl.multiple_of((yy * 2 + cc) * tall, 8)
+        start = pl.multiple_of((cc * 2 + yy) * tall, 8)
         ref[...] = sum_ref[pl.ds(start, tall), :]
 
 
@@ -203,10 +212,6 @@
 
 def swapped(value, axis):
     return lax.ppermute(value, axis, [(0, 1), (1, 0)])
-
-
-def turned(value, j):
-    return lax.ppermute(value, Q, [(q, q ^ j) for q in range(4)])
 
 
 def exchanged(value, axis):
@@ -223,7 +228,7 @@
     rows = cands * rank
     width = depth // groups
     block = up8(own)
-    lanes = upl(nq * block + PARTS * tok + 3)
+    tall = block + PARTS * tok
     shape = jax.ShapeDtypeStruct
 
     cut = call(cut_a, shape((groups, rows, width), BF16), (factor_a,), 1 << 20)
@@ -231,30 +236,33 @@
 
     packed = call(
         pack_b,
-        shape((nz, rows, lanes), BF16),
+        shape((nz * 2, rows, layout(own, tok)[-1]), BF16),
         (fitness, window, factor_a, factor_b),
         1 << 24,
         scratch=[pltpu.VMEM((rows, upl(hidden) + 2 * LANE), F32)],
         smem=(0,),
     )
-    columns = exchanged(packed, "z")
-    tall = block + PARTS * tok
-    weighted, *pieces = call(
-        turn_b,
-        [shape((groups, nq * block, nz * rows), BF16)] + [shape((tall, nz * rows), BF16)] * nq,
+    columns = exchanged(packed, ("z", "core"))
+    weighted, keep, send = call(
+        functools.partial(turn_b, own, tok),
+        [
+            shape((groups * 2, 2 * block, nz * rows), BF16),
+            shape((tall, 2 * nz * rows), BF16),
+            shape((tall, 2 * nz * rows), BF16),
+        ],
         (columns,),
         1 << 24,
-        scratch=[pltpu.VMEM((nq * block, nz * rows), BF16)],
-    )
-    weighted = exchanged(weighted, "grp")
-    pieces[1:] = [turned(pieces[j], j) for j in range(1, nq)]
+        scratch=[pltpu.VMEM((2, tall, 2 * nz * rows), BF16)],
+    )
+    weighted = exchanged(weighted, ("grp", "core"))
+    got = swapped(send, "yhi")
     base = call(base_rows, shape((own, LANE), F32), (weight, window), 1 << 28)
     perturbed = call(
         functools.partial(perturb, 0.25 / math.sqrt(depth)),
         shape((own, cands * nz * nq * tok), BF16),
-        (base, *pieces),
+        (base, keep, got),
         1 << 30,
-        scratch=[pltpu.VMEM((nq, tall, nz * rows), BF16)],
+        scratch=[pltpu.VMEM((2, tall, 2 * nz * rows), BF16)],
     )
 
     mine = mine[None]

time: 123 us -> 124 us (level)
  the two profiles are of different devices: /device:TPU:99 before, /device:TPU:34 now
where the time goes in v2:
time: 124 us; the launch traced here: 123 us
  starting transfers between devices  62 us (50%)
  waiting for transfers between devices  48.5 us (39%)
  Pallas kernels  6.85 us (6%)
  local copies, waits for them, and re-layouts  4.16 us (3%)
    all_to_all x3, starting transfers between devices, exchanged(): return lax.all_to_all(value, axis, 0, 0, tiled=True)  26 us
    ppermute x7, starting transfers between devices, shifted(): return lax.ppermute(value, 'z', [(i, (i - offset) % n) for i in range(n)])  24.4 us
    all_to_all x3, waiting for transfers between devices, exchanged(): return lax.all_to_all(value, axis, 0, 0, tiled=True)  20.5 us
    ppermute x7, waiting for transfers between devices, shifted(): return lax.ppermute(value, 'z', [(i, (i - offset) % n) for i in range(n)])  19.9 us
    ppermute x4, starting transfers between devices, swapped(): return lax.ppermute(value, axis, [(0, 1), (1, 0)])  11.7 us
    ppermute x4, waiting for transfers between devices, swapped(): return lax.ppermute(value, axis, [(0, 1), (1, 0)])  8.1 us
    pallas_call x6, Pallas kernels, call(): pl.pallas_call(body, out_shape=out_shape, in_specs=[scalar if i in smem e...  6.85 us
    unnamed x14, local copies, waits for them, and re-layouts  4.16 us
  transfers between devices with their start and end apart: 14, of which 7 were waited for; matrix products, arithmetic and copies ran while one was open for 0% of the time, Pallas kernels for 3%

profile of v2, /device:TPU:34, one launch (start us, length us, event | category | flops | bytes accessed | tf_op | source)
XLA Modules:
  0.0 123.3 jit_solution(475154976805388160)
XLA Ops:
  0.6 0.0 copy-start.1
  0.6 0.9 copy-done.1
  1.5 0.0 copy-start.3
  1.5 0.8 copy-done.3
  2.4 0.0 copy-start.5
  2.4 0.9 copy-done.5
  3.3 0.0 copy-start.6
  3.3 0.7 copy-done.6
  4.0 1.5 %shard_map.69 = bf16[32,8,384]{2,1,0:T(8,128)(2,1)} custom-call(f32[2]{0:T(128)S(1)} %copy-done.6, bf16[16,4096]{1,0:T(8,128)(2,1)S(1)} %copy-done.1, bf16[2,4,4096]{2,1,0:T(4,128)(2,1)S(1)} %copy-done.3, bf16[2,4,11008]{2,1,0:T(4,128)(2,1)S(1)} %copy-done.5), custom_call_target="tpu_custom_call" | custom-call | flops 16777216 | bytes 1048576 | tf_op jit(solution)/shard_map/pallas_call | solution.py:33
  5.5 15.4 %all-to-all-start = ((bf16[32,8,384]{2,1,0:T(8,128)(2,1)}), bf16[32,8,384]{2,1,0:T(8,128)(2,1)S(1)}, u32[]{:S(2)}, u32[]{:S(2)}) async-start(bf16[32,8,384]{2,1,0:T(8,128)(2,1)} %shard_map.69), calls=%async_computation | async-start | bytes 393216 | tf_op jit(solution)/shard_map/all_to_all | solution.py:218
  20.8 0.0 copy-start.4
  20.9 0.8 copy-done.4
  21.7 0.6 shard_map.72
  22.3 16.8 %all-to-all-done.in_ref = bf16[32,8,384]{2,1,0:T(8,128)(2,1)S(1)} async-done(((bf16[32,8,384]{2,1,0:T(8,128)(2,1)}), bf16[32,8,384]{2,1,0:T(8,128)(2,1)S(1)}, u32[]{:S(2)}, u32[]{:S(2)}) %all-to-all-start) | async-done | bytes 196640 | tf_op jit(solution)/shard_map/all_to_all | solution.py:218
  39.2 5.8 %all-to-all-start.2 = ((bf16[8,8,512]{2,1,0:T(8,128)(2,1)}), bf16[8,8,512]{2,1,0:T(8,128)(2,1)S(1)}, u32[]{:S(2)}, u32[]{:S(2)}) async-start(bf16[8,8,512]{2,1,0:T(8,128)(2,1)} %shard_map.72), calls=%async_computation.2 | async-start | bytes 131072 | tf_op jit(solution)/shard_map/all_to_all | solution.py:218
  45.0 1.4 %shard_map.70 = (bf16[16,352,128]{2,1,0:T(8,128)(2,1)}, bf16[208,256]{1,0:T(8,128)(2,1)S(1)}, bf16[208,256]{1,0:T(8,128)(2,1)S(1)}) custom-call(bf16[32,8,384]{2,1,0:T(8,128)(2,1)S(1)} %all-to-all-done.in_ref), custom_call_target="tpu_custom_call" | custom-call | flops 16777216 | bytes 1048576 | tf_op jit(solution)/shard_map/pallas_call | solution.py:33
  46.4 3.7 %all-to-all-done.2 = bf16[8,8,512]{2,1,0:T(8,128)(2,1)S(1)} async-done(((bf16[8,8,512]{2,1,0:T(8,128)(2,1)}), bf16[8,8,512]{2,1,0:T(8,128)(2,1)S(1)}, u32[]{:S(2)}, u32[]{:S(2)}) %all-to-all-start.2) | async-done | bytes 65568 | tf_op jit(solution)/shard_map/all_to_all | solution.py:218
  50.1 4.8 %all-to-all-start.1 = ((bf16[16,352,128]{2,1,0:T(8,128)(2,1)}), bf16[16,352,128]{2,1,0:T(8,128)(2,1)S(1)}, u32[]{:S(2)}, u32[]{:S(2)}) async-start(bf16[16,352,128]{2,1,0:T(8,128)(2,1)} %get-tuple-element.11), calls=%async_computation.1 | async-start | bytes 2883584 | tf_op jit(solution)/shard_map/all_to_all | solution.py:218
  54.9 3.5 %collective-permute-start.1 = (bf16[1,8,8,512]{3,2,1,0:T(8,128)(2,1)S(1)}, bf16[1,8,8,512]{3,2,1,0:T(8,128)(2,1)S(1)}, u32[]{:S(2)}, u32[]{:S(2)}) collective-permute-start(bf16[1,8,8,512]{3,2,1,0:T(8,128)(2,1)S(1)} %bitcast.1), channel_id=1, source_target_pairs={{0,44},{4,48},{8,52},{12,56},{16,60},{20,0},{24,4},{28,8},{32,12},... | collective-permute-start | bytes 196616 | tf_op jit(solution)/shard_map/ppermute | solution.py:210
  58.4 7.1 %collective-permute-start.2 = (bf16[1,8,8,512]{3,2,1,0:T(8,128)(2,1)S(1)}, bf16[1,8,8,512]{3,2,1,0:T(8,128)(2,1)S(1)}, u32[]{:S(2)}, u32[]{:S(2)}) collective-permute-start(bf16[1,8,8,512]{3,2,1,0:T(8,128)(2,1)S(1)} %bitcast.2), channel_id=1, source_target_pairs={{0,20},{4,24},{8,28},{12,32},{16,36},{20,40},{24,44},{28,48},{32,5... | collective-permute-start | bytes 196616 | tf_op jit(solution)/shard_map/ppermute | solution.py:210
  65.5 4.6 %collective-permute-done.1 = bf16[1,8,8,512]{3,2,1,0:T(8,128)(2,1)S(1)} collective-permute-done((bf16[1,8,8,512]{3,2,1,0:T(8,128)(2,1)S(1)}, bf16[1,8,8,512]{3,2,1,0:T(8,128)(2,1)S(1)}, u32[]{:S(2)}, u32[]{:S(2)}) %collective-permute-start.1) | collective-permute-done | bytes 65568 | tf_op jit(solution)/shard_map/ppermute | solution.py:210
  70.1 4.4 %collective-permute-done.2 = bf16[1,8,8,512]{3,2,1,0:T(8,128)(2,1)S(1)} collective-permute-done((bf16[1,8,8,512]{3,2,1,0:T(8,128)(2,1)S(1)}, bf16[1,8,8,512]{3,2,1,0:T(8,128)(2,1)S(1)}, u32[]{:S(2)}, u32[]{:S(2)}) %collective-permute-start.2) | collective-permute-done | bytes 65568 | tf_op jit(solution)/shard_map/ppermute | solution.py:210
  74.6 0.0 copy-start.2
  74.6 2.1 %collective-permute-start.3 = (bf16[3,8,8,512]{3,2,1,0:T(8,128)(2,1)S(1)}, bf16[3,8,8,512]{3,2,1,0:T(8,128)(2,1)S(1)}, u32[]{:S(2)}, u32[]{:S(2)}) collective-permute-start(bf16[3,8,8,512]{3,2,1,0:T(8,128)(2,1)S(1)} %pad_maximum_fusion.refs_1_), channel_id=1, source_target_pairs={{0,60},{4,0},{8,4},{12,8},{16,12},{20,16},{24,20},{28,24},{32,28},... | collective-permute-start | bytes 589832 | tf_op jit(solution)/shard_map/ppermute | solution.py:210
  76.6 3.9 %collective-permute-start.4 = (bf16[3,8,8,512]{3,2,1,0:T(8,128)(2,1)S(1)}, bf16[3,8,8,512]{3,2,1,0:T(8,128)(2,1)S(1)}, u32[]{:S(2)}, u32[]{:S(2)}) collective-permute-start(bf16[3,8,8,512]{3,2,1,0:T(8,128)(2,1)S(1)} %pad_maximum_fusion.refs_1_), channel_id=1, source_target_pairs={{0,4},{4,8},{8,12},{12,16},{16,20},{20,24},{24,28},{28,32},{32,36}... | collective-permute-start | bytes 589832 | tf_op jit(solution)/shard_map/ppermute | solution.py:210
  80.6 2.8 %collective-permute-done.3.refs_2_ = bf16[3,8,8,512]{3,2,1,0:T(8,128)(2,1)S(1)} collective-permute-done((bf16[3,8,8,512]{3,2,1,0:T(8,128)(2,1)S(1)}, bf16[3,8,8,512]{3,2,1,0:T(8,128)(2,1)S(1)}, u32[]{:S(2)}, u32[]{:S(2)}) %collective-permute-start.3) | collective-permute-done | bytes 196640 | tf_op jit(solution)/shard_map/ppermute | solution.py:210
  83.4 2.2 %collective-permute-start.5 = (bf16[3,8,8,512]{3,2,1,0:T(8,128)(2,1)S(1)}, bf16[3,8,8,512]{3,2,1,0:T(8,128)(2,1)S(1)}, u32[]{:S(2)}, u32[]{:S(2)}) collective-permute-start(bf16[3,8,8,512]{3,2,1,0:T(8,128)(2,1)S(1)} %collective-permute-done.3.refs_2_), channel_id=1, source_target_pairs={{0,60},{4,0},{8,4},{12,8},{16,12},{20,16},{24,20},{28,24},{32,28},... | collective-permute-start | bytes 589832 | tf_op jit(solution)/shard_map/ppermute | solution.py:210
  85.6 0.0 collective-permute-done.4.refs_3_
  85.6 3.6 %collective-permute-start.6 = (bf16[3,8,8,512]{3,2,1,0:T(8,128)(2,1)S(1)}, bf16[3,8,8,512]{3,2,1,0:T(8,128)(2,1)S(1)}, u32[]{:S(2)}, u32[]{:S(2)}) collective-permute-start(bf16[3,8,8,512]{3,2,1,0:T(8,128)(2,1)S(1)} %collective-permute-done.4.refs_3_), channel_id=1, source_target_pairs={{0,4},{4,8},{8,12},{12,16},{16,20},{20,24},{24,28},{28,32},{32,36}... | collective-permute-start | bytes 589832 | tf_op jit(solution)/shard_map/ppermute | solution.py:210
  89.2 1.9 %collective-permute-start.7 = (bf16[1,8,8,512]{3,2,1,0:T(8,128)(2,1)S(1)}, bf16[1,8,8,512]{3,2,1,0:T(8,128)(2,1)S(1)}, u32[]{:S(2)}, u32[]{:S(2)}) collective-permute-start(bf16[1,8,8,512]{3,2,1,0:T(8,128)(2,1)S(1)} %collective-permute-done.1), channel_id=1, source_target_pairs={{0,52},{4,56},{8,60},{12,0},{16,4},{20,8},{24,12},{28,16},{32,20},... | collective-permute-start | bytes 196616 | tf_op jit(solution)/shard_map/ppermute | solution.py:210
  91.2 8.1 %collective-permute-done.7.refs_6_ = bf16[1,8,8,512]{3,2,1,0:T(8,128)(2,1)S(1)} collective-permute-done((bf16[1,8,8,512]{3,2,1,0:T(8,128)(2,1)S(1)}, bf16[1,8,8,512]{3,2,1,0:T(8,128)(2,1)S(1)}, u32[]{:S(2)}, u32[]{:S(2)}) %collective-permute-start.7) | collective-permute-done | bytes 65568 | tf_op jit(solution)/shard_map/ppermute | solution.py:210
  99.2 0.0 collective-permute-done.5.refs_4_
  99.3 0.0 collective-permute-done.6.refs_5_
  99.3 0.0 all-to-all-done.1.refs_0_
  99.3 0.0 copy-start
  99.3 1.1 shard_map.73
  100.4 1.9 %collective-permute-start.9 = (f32[176,512]{1,0:T(8,128)S(1)}, f32[176,512]{1,0:T(8,128)S(1)}, u32[]{:S(2)}, u32[]{:S(2)}) collective-permute-start(f32[176,512]{1,0:T(8,128)S(1)} %get-tuple-element.15), channel_id=1, source_target_pairs={{0,1},{1,0},{2,3},{3,2},{4,5},{5,4},{6,7},{7,6},{8,9},{9,8},{10,11... | collective-permute-start | bytes 1081352 | tf_op jit(solution)/shard_map/ppermute | solution.py:214
  102.3 2.4 %collective-permute-start.8 = (f32[176,512]{1,0:T(8,128)S(1)}, f32[176,512]{1,0:T(8,128)S(1)}, u32[]{:S(2)}, u32[]{:S(2)}) collective-permute-start(f32[176,512]{1,0:T(8,128)S(1)} %get-tuple-element.13), channel_id=1, source_target_pairs={{0,1},{1,0},{2,3},{3,2},{4,5},{5,4},{6,7},{7,6},{8,9},{9,8},{10,11... | collective-permute-start | bytes 1081352 | tf_op jit(solution)/shard_map/ppermute | solution.py:214
  104.7 0.0 collective-permute-done.9
  104.7 0.1 add.10
  104.8 4.8 %collective-permute-start.10 = (f32[176,512]{1,0:T(8,128)S(1)}, f32[176,512]{1,0:T(8,128)S(1)}, u32[]{:S(2)}, u32[]{:S(2)}) collective-permute-start(f32[176,512]{1,0:T(8,128)S(1)} %add.10), channel_id=1, source_target_pairs={{0,2},{2,0},{1,3},{3,1},{4,6},{6,4},{5,7},{7,5},{8,10},{10,8},{9,1... | collective-permute-start | bytes 1081352 | tf_op jit(solution)/shard_map/ppermute | solution.py:214
  109.6 2.5 %collective-permute-start = (bf16[208,256]{1,0:T(8,128)(2,1)S(1)}, bf16[208,256]{1,0:T(8,128)(2,1)S(1)}, u32[]{:S(2)}, u32[]{:S(2)}) collective-permute-start(bf16[208,256]{1,0:T(8,128)(2,1)S(1)} %get-tuple-element.10), channel_id=1, source_target_pairs={{0,2},{2,0},{1,3},{3,1},{4,6},{6,4},{5,7},{7,5},{8,10},{10,8},{9,1... | collective-permute-start | bytes 319496 | tf_op jit(solution)/shard_map/ppermute | solution.py:214
  112.2 0.0 copy-done.2
  112.2 0.0 copy-done
  112.2 0.5 shard_map.68.base_ref
  112.7 8.1 %collective-permute-done.got_ref = bf16[208,256]{1,0:T(8,128)(2,1)S(1)} collective-permute-done((bf16[208,256]{1,0:T(8,128)(2,1)S(1)}, bf16[208,256]{1,0:T(8,128)(2,1)S(1)}, u32[]{:S(2)}, u32[]{:S(2)}) %collective-permute-start) | collective-permute-done | bytes 106528 | tf_op jit(solution)/shard_map/ppermute | solution.py:214
  120.8 1.7 %shard_map.71 = bf16[172,2048]{1,0:T(8,128)(2,1)} custom-call(f32[172,128]{1,0:T(8,128)S(1)} %shard_map.68.base_ref, bf16[208,256]{1,0:T(8,128)(2,1)S(1)} %get-tuple-element.9.keep_ref, bf16[208,256]{1,0:T(8,128)(2,1)S(1)} %collective-permute-done.got_ref), custom_call_target="tpu_custom_call" | custom-call | flops 1073741824 | bytes 1048576 | tf_op jit(solution)/shard_map/pallas_call | solution.py:33
  122.5 0.0 collective-permute-done.8
  122.5 0.0 collective-permute-done.10
  122.5 0.8 fusion
  (1 shorter events, 0.0 us)
Async XLA Ops:
  0.6 0.9 copy-start.1
  1.5 0.8 copy-start.3
  2.4 0.9 copy-start.5
  3.3 0.7 copy-start.6
  5.5 33.7 %all-to-all-start = ((bf16[32,8,384]{2,1,0:T(8,128)(2,1)}), bf16[32,8,384]{2,1,0:T(8,128)(2,1)S(1)}, u32[]{:S(2)}, u32[]{:S(2)}) async-start(bf16[32,8,384]{2,1,0:T(8,128)(2,1)} %shard_map.69), calls=%async_computation | async-start | bytes 393216 | tf_op jit(solution)/shard_map/all_to_all | solution.py:218
  20.8 0.8 copy-start.4
  39.2 10.9 %all-to-all-start.2 = ((bf16[8,8,512]{2,1,0:T(8,128)(2,1)}), bf16[8,8,512]{2,1,0:T(8,128)(2,1)S(1)}, u32[]{:S(2)}, u32[]{:S(2)}) async-start(bf16[8,8,512]{2,1,0:T(8,128)(2,1)} %shard_map.72), calls=%async_computation.2 | async-start | bytes 131072 | tf_op jit(solution)/shard_map/all_to_all | solution.py:218
  50.1 49.2 %all-to-all-start.1 = ((bf16[16,352,128]{2,1,0:T(8,128)(2,1)}), bf16[16,352,128]{2,1,0:T(8,128)(2,1)S(1)}, u32[]{:S(2)}, u32[]{:S(2)}) async-start(bf16[16,352,128]{2,1,0:T(8,128)(2,1)} %get-tuple-element.11), calls=%async_computation.1 | async-start | bytes 2883584 | tf_op jit(solution)/shard_map/all_to_all | solution.py:218
  54.9 15.3 %collective-permute-start.1 = (bf16[1,8,8,512]{3,2,1,0:T(8,128)(2,1)S(1)}, bf16[1,8,8,512]{3,2,1,0:T(8,128)(2,1)S(1)}, u32[]{:S(2)}, u32[]{:S(2)}) collective-permute-start(bf16[1,8,8,512]{3,2,1,0:T(8,128)(2,1)S(1)} %bitcast.1), channel_id=1, source_target_pairs={{0,44},{4,48},{8,52},{12,56},{16,60},{20,0},{24,4},{28,8},{32,12},... | collective-permute-start | bytes 196616 | tf_op jit(solution)/shard_map/ppermute | solution.py:210
  58.4 16.2 %collective-permute-start.2 = (bf16[1,8,8,512]{3,2,1,0:T(8,128)(2,1)S(1)}, bf16[1,8,8,512]{3,2,1,0:T(8,128)(2,1)S(1)}, u32[]{:S(2)}, u32[]{:S(2)}) collective-permute-start(bf16[1,8,8,512]{3,2,1,0:T(8,128)(2,1)S(1)} %bitcast.2), channel_id=1, source_target_pairs={{0,20},{4,24},{8,28},{12,32},{16,36},{20,40},{24,44},{28,48},{32,5... | collective-permute-start | bytes 196616 | tf_op jit(solution)/shard_map/ppermute | solution.py:210
  74.6 37.6 %copy-start.2 = (bf16[16,4096]{1,0:T(8,128)(2,1)S(1)}, bf16[16,4096]{1,0:T(8,128)(2,1)}, u32[]{:S(2)}) copy-start(bf16[16,4096]{1,0:T(8,128)(2,1)} %win_ref.3) | copy-start | bytes 393220
  74.6 8.8 %collective-permute-start.3 = (bf16[3,8,8,512]{3,2,1,0:T(8,128)(2,1)S(1)}, bf16[3,8,8,512]{3,2,1,0:T(8,128)(2,1)S(1)}, u32[]{:S(2)}, u32[]{:S(2)}) collective-permute-start(bf16[3,8,8,512]{3,2,1,0:T(8,128)(2,1)S(1)} %pad_maximum_fusion.refs_1_), channel_id=1, source_target_pairs={{0,60},{4,0},{8,4},{12,8},{16,12},{20,16},{24,20},{28,24},{32,28},... | collective-permute-start | bytes 589832 | tf_op jit(solution)/shard_map/ppermute | solution.py:210
  76.6 8.9 %collective-permute-start.4 = (bf16[3,8,8,512]{3,2,1,0:T(8,128)(2,1)S(1)}, bf16[3,8,8,512]{3,2,1,0:T(8,128)(2,1)S(1)}, u32[]{:S(2)}, u32[]{:S(2)}) collective-permute-start(bf16[3,8,8,512]{3,2,1,0:T(8,128)(2,1)S(1)} %pad_maximum_fusion.refs_1_), channel_id=1, source_target_pairs={{0,4},{4,8},{8,12},{12,16},{16,20},{20,24},{24,28},{28,32},{32,36}... | collective-permute-start | bytes 589832 | tf_op jit(solution)/shard_map/ppermute | solution.py:210
  83.4 15.9 %collective-permute-start.5 = (bf16[3,8,8,512]{3,2,1,0:T(8,128)(2,1)S(1)}, bf16[3,8,8,512]{3,2,1,0:T(8,128)(2,1)S(1)}, u32[]{:S(2)}, u32[]{:S(2)}) collective-permute-start(bf16[3,8,8,512]{3,2,1,0:T(8,128)(2,1)S(1)} %collective-permute-done.3.refs_2_), channel_id=1, source_target_pairs={{0,60},{4,0},{8,4},{12,8},{16,12},{20,16},{24,20},{28,24},{32,28},... | collective-permute-start | bytes 589832 | tf_op jit(solution)/shard_map/ppermute | solution.py:210
  85.6 13.7 %collective-permute-start.6 = (bf16[3,8,8,512]{3,2,1,0:T(8,128)(2,1)S(1)}, bf16[3,8,8,512]{3,2,1,0:T(8,128)(2,1)S(1)}, u32[]{:S(2)}, u32[]{:S(2)}) collective-permute-start(bf16[3,8,8,512]{3,2,1,0:T(8,128)(2,1)S(1)} %collective-permute-done.4.refs_3_), channel_id=1, source_target_pairs={{0,4},{4,8},{8,12},{12,16},{16,20},{20,24},{24,28},{28,32},{32,36}... | collective-permute-start | bytes 589832 | tf_op jit(solution)/shard_map/ppermute | solution.py:210
  89.2 10.0 %collective-permute-start.7 = (bf16[1,8,8,512]{3,2,1,0:T(8,128)(2,1)S(1)}, bf16[1,8,8,512]{3,2,1,0:T(8,128)(2,1)S(1)}, u32[]{:S(2)}, u32[]{:S(2)}) collective-permute-start(bf16[1,8,8,512]{3,2,1,0:T(8,128)(2,1)S(1)} %collective-permute-done.1), channel_id=1, source_target_pairs={{0,52},{4,56},{8,60},{12,0},{16,4},{20,8},{24,12},{28,16},{32,20},... | collective-permute-start | bytes 196616 | tf_op jit(solution)/shard_map/ppermute | solution.py:210
  99.3 12.9 %copy-start = (bf16[172,4096]{1,0:T(8,128)(2,1)S(1)}, bf16[172,4096]{1,0:T(8,128)(2,1)}, u32[]{:S(2)}) copy-start(bf16[172,4096]{1,0:T(8,128)(2,1)} %weight_ref.1) | copy-start | bytes 4227076
  100.4 4.3 %collective-permute-start.9 = (f32[176,512]{1,0:T(8,128)S(1)}, f32[176,512]{1,0:T(8,128)S(1)}, u32[]{:S(2)}, u32[]{:S(2)}) collective-permute-start(f32[176,512]{1,0:T(8,128)S(1)} %get-tuple-element.15), channel_id=1, source_target_pairs={{0,1},{1,0},{2,3},{3,2},{4,5},{5,4},{6,7},{7,6},{8,9},{9,8},{10,11... | collective-permute-start | bytes 1081352 | tf_op jit(solution)/shard_map/ppermute | solution.py:214
  102.3 20.1 %collective-permute-start.8 = (f32[176,512]{1,0:T(8,128)S(1)}, f32[176,512]{1,0:T(8,128)S(1)}, u32[]{:S(2)}, u32[]{:S(2)}) collective-permute-start(f32[176,512]{1,0:T(8,128)S(1)} %get-tuple-element.13), channel_id=1, source_target_pairs={{0,1},{1,0},{2,3},{3,2},{4,5},{5,4},{6,7},{7,6},{8,9},{9,8},{10,11... | collective-permute-start | bytes 1081352 | tf_op jit(solution)/shard_map/ppermute | solution.py:214
  104.8 17.7 %collective-permute-start.10 = (f32[176,512]{1,0:T(8,128)S(1)}, f32[176,512]{1,0:T(8,128)S(1)}, u32[]{:S(2)}, u32[]{:S(2)}) collective-permute-start(f32[176,512]{1,0:T(8,128)S(1)} %add.10), channel_id=1, source_target_pairs={{0,2},{2,0},{1,3},{3,1},{4,6},{6,4},{5,7},{7,5},{8,10},{10,8},{9,1... | collective-permute-start | bytes 1081352 | tf_op jit(solution)/shard_map/ppermute | solution.py:214
  109.6 11.2 %collective-permute-start = (bf16[208,256]{1,0:T(8,128)(2,1)S(1)}, bf16[208,256]{1,0:T(8,128)(2,1)S(1)}, u32[]{:S(2)}, u32[]{:S(2)}) collective-permute-start(bf16[208,256]{1,0:T(8,128)(2,1)S(1)} %get-tuple-element.10), channel_id=1, source_target_pairs={{0,2},{2,0},{1,3},{3,1},{4,6},{6,4},{5,7},{7,5},{8,10},{10,8},{9,1... | collective-permute-start | bytes 319496 | tf_op jit(solution)/shard_map/ppermute | solution.py:214

commit v3 on v2

--- a/solution.py
+++ b/solution.py
@@ -26,18 +26,21 @@
     return (n + LANE - 1) // LANE * LANE
 
 
-def call(body, out_shape, args, flops, scratch=(), smem=()):
+def call(body, out_shape, args, flops, scratch=(), smem=(), far=()):
     vmem = pl.BlockSpec(memory_space=pltpu.VMEM)
     scalar = pl.BlockSpec(memory_space=pltpu.SMEM)
     many = isinstance(out_shape, (list, tuple))
     return pl.pallas_call(
         body,
         out_shape=out_shape,
-        in_specs=[scalar if i in smem else vmem for i in range(len(args))],
+        in_specs=[
+            scalar if i in smem else pl.BlockSpec(memory_space=pltpu.HBM) if i in far else vmem
+            for i in range(len(args))
+        ],
         out_specs=[vmem] * len(out_shape) if many else vmem,
         scratch_shapes=list(scratch),
         cost_estimate=pl.CostEstimate(flops=flops, bytes_accessed=1 << 20, transcendentals=0),
-        compiler_params=pltpu.CompilerParams(vmem_limit_bytes=16 << 20),
+        compiler_params=pltpu.CompilerParams(vmem_limit_bytes=(60 if far else 16) << 20),
     )(*args)
 
 
@@ -48,7 +51,10 @@
     return hi, mid, (rest - mid).astype(BF16).astype(F32)
 
 
-def cut_a(a_ref, out_ref):
+def cut_a(a_hbm, out_ref, a_ref, sem):
+    load = pltpu.make_async_copy(a_hbm, a_ref, sem)
+    load.start()
+    load.wait()
     groups, _, width = out_ref.shape
     cands = a_ref.shape[0]
     for g in range(groups):
@@ -63,7 +69,17 @@
     return first, second, second + own, upl(second + own + 3)
 
 
-def pack_b(fit_ref, win_ref, a_ref, b_ref, out_ref, wide_ref):
+def pack_b(fit_ref, win_hbm, a_hbm, b_hbm, out_ref, wide_ref, win_ref, a_ref, b_ref, sems):
+    loads = [
+        pltpu.make_async_copy(source, target, sems.at[i])
+        for i, (source, target) in enumerate(
+            ((b_hbm, b_ref), (a_hbm, a_ref), (win_hbm, win_ref))
+        )
+    ]
+    for load in loads:
+        load.start()
+    for load in loads:
+        load.wait()
     blocks, rows, lanes = out_ref.shape
     cands, rank, hidden = b_ref.shape
     tok, depth = win_ref.shape
@@ -184,25 +200,43 @@
 OFFSETS = ((0, 5, -5), (1, 6, -4), (-1, 4, -6), (2, 7, -3), (-2, 3, -7), (8,))
 
 
-def update_parts(*refs):
-    w_ref, chunks, out_refs = refs[0], refs[1:7], refs[7:11]
-    rows_ref, sum_ref = refs[11:]
-    groups, nz, rows, width = rows_ref.shape
-    z, y, core = (lax.axis_index(name) for name in SHARD)
+def place_rows(chunks, rows_ref):
+    groups, nz, _, _ = rows_ref.shape
+    z = lax.axis_index("z")
     for ref, offsets in zip(chunks, OFFSETS):
         for i, offset in enumerate(offsets):
             place = lax.rem(z + offset + nz, nz)
             for g in range(groups):
                 rows_ref[g, place] = ref[i, g]
+
+
+def update_first(w_ref, *refs):
+    chunks, out_ref, rows_ref = refs[:6], refs[6], refs[7]
+    groups, nz, rows, width = rows_ref.shape
+    place_rows(chunks, rows_ref)
+    y, core = lax.axis_index("yhi"), lax.axis_index("core")
+    tall = out_ref.shape[0]
+    start = pl.multiple_of((1 - y) * tall, 8)
     left = jnp.concatenate(
-        [jnp.concatenate([w_ref[2 * g + c] for g in range(groups)], axis=1) for c in range(2)], axis=0
+        [w_ref[2 * g + 1 - core, pl.ds(start, tall), :] for g in range(groups)], axis=1
     )
     right = rows_ref[...].reshape(groups * nz * rows, width)
-    sum_ref[...] = jnp.dot(left, right, preferred_element_type=F32)
+    out_ref[...] = jnp.dot(left, right, preferred_element_type=F32)
+
+
+def update_rest(w_ref, *refs):
+    chunks, out_refs, rows_ref = refs[:6], refs[6:9], refs[9]
+    groups, nz, rows, width = rows_ref.shape
+    place_rows(chunks, rows_ref)
+    y, core = lax.axis_index("yhi"), lax.axis_index("core")
     tall = out_refs[0].shape[0]
-    for ref, yy, cc in zip(out_refs, (y, y, 1 - y, 1 - y), (core, 1 - core, core, 1 - core)):
-        start = pl.multiple_of((cc * 2 + yy) * tall, 8)
-        ref[...] = sum_ref[pl.ds(start, tall), :]
+    right = rows_ref[...].reshape(groups * nz * rows, width)
+    for ref, yy, cc in zip(out_refs, (1 - y, y, y), (core, core, 1 - core)):
+        start = pl.multiple_of(yy * tall, 8)
+        left = jnp.concatenate(
+            [w_ref[2 * g + cc, pl.ds(start, tall), :] for g in range(groups)], axis=1
+        )
+        ref[...] = jnp.dot(left, right, preferred_element_type=F32)
 
 
 def shifted(value, offset):
@@ -231,7 +265,14 @@
     tall = block + PARTS * tok
     shape = jax.ShapeDtypeStruct
 
-    cut = call(cut_a, shape((groups, rows, width), BF16), (factor_a,), 1 << 20)
+    cut = call(
+        cut_a,
+        shape((groups, rows, width), BF16),
+        (factor_a,),
+        1 << 20,
+        scratch=[pltpu.VMEM(factor_a.shape, BF16), pltpu.SemaphoreType.DMA],
+        far=(0,),
+    )
     mine = exchanged(cut, "grp")
 
     packed = call(
@@ -239,8 +280,15 @@
         shape((nz * 2, rows, layout(own, tok)[-1]), BF16),
         (fitness, window, factor_a, factor_b),
         1 << 24,
-        scratch=[pltpu.VMEM((rows, upl(hidden) + 2 * LANE), F32)],
+        scratch=[
+            pltpu.VMEM((rows, upl(hidden) + 2 * LANE), F32),
+            pltpu.VMEM(window.shape, BF16),
+            pltpu.VMEM(factor_a.shape, BF16),
+            pltpu.VMEM(factor_b.shape, BF16),
+            pltpu.SemaphoreType.DMA((3,)),
+        ],
         smem=(0,),
+        far=(1, 2, 3),
     )
     columns = exchanged(packed, ("z", "core"))
     weighted, keep, send = call(
@@ -272,16 +320,10 @@
     up2, down2 = shifted(up, 1), shifted(down, -1)
     across = shifted(far, 3)
     part = shape((block, width), F32)
-    oo, ox, xo, xx = call(
-        update_parts,
-        [part] * 4,
-        (weighted, near, up, down, up2, down2, across),
-        1 << 30,
-        scratch=[
-            pltpu.VMEM((groups, nz, rows, width), BF16),
-            pltpu.VMEM((nq * block, width), F32),
-        ],
-    )
+    operands = (weighted, near, up, down, up2, down2, across)
+    held = [pltpu.VMEM((groups, nz, rows, width), BF16)]
+    xx = call(update_first, part, operands, 1 << 28, scratch=held)
+    xo, oo, ox = call(update_rest, [part] * 3, operands, 1 << 29, scratch=held)
     there = xo + swapped(xx, "core")
     here = oo + swapped(ox, "core")
     update = (here + swapped(there, "yhi"))[:own] * (0.5 / math.sqrt(total))

time: 124 us -> 122 us (0.984)
  local copies, waits for them, and re-layouts: 4.16 us -> 0.01 us
  Pallas kernels: 6.85 us -> 9.01 us
    unnamed x14 -> x4, local copies, waits for them, and re-layouts: 4.16 us -> 0.01 us
    pallas_call x6 -> x7, Pallas kernels: 6.85 us -> 9.01 us  [call(): pl.pallas_call(body, out_shape=out_shape, in_specs=[scalar if i in smem e...]
  transfers between devices with their start and end apart: 14 -> 14, of which waited for: 7 -> 7; matrix products, arithmetic and copies ran while one was open for 0% -> 0% of each run, Pallas kernels for 3% -> 5%
where the time goes in v3:
time: 122 us; the launch traced here: 121 us
  starting transfers between devices  62 us (51%)
  waiting for transfers between devices  48.6 us (40%)
  Pallas kernels  9.01 us (7%)
    all_to_all x3, starting transfers between devices, exchanged(): return lax.all_to_all(value, axis, 0, 0, tiled=True)  26 us
    ppermute x7, starting transfers between devices, shifted(): return lax.ppermute(value, 'z', [(i, (i - offset) % n) for i in range(n)])  24.2 us
    all_to_all x3, waiting for transfers between devices, exchanged(): return lax.all_to_all(value, axis, 0, 0, tiled=True)  20.5 us
    ppermute x7, waiting for transfers between devices, shifted(): return lax.ppermute(value, 'z', [(i, (i - offset) % n) for i in range(n)])  19.9 us
    ppermute x4, starting transfers between devices, swapped(): return lax.ppermute(value, axis, [(0, 1), (1, 0)])  11.8 us
    pallas_call x7, Pallas kernels, call(): pl.pallas_call(body, out_shape=out_shape, in_specs=[scalar if i in smem e...  9.01 us
    ppermute x4, waiting for transfers between devices, swapped(): return lax.ppermute(value, axis, [(0, 1), (1, 0)])  8.11 us
  transfers between devices with their start and end apart: 14, of which 7 were waited for; matrix products, arithmetic and copies ran while one was open for 0% of the time, Pallas kernels for 5%

profile of v3, /device:TPU:34, one launch (start us, length us, event | category | flops | bytes accessed | tf_op | source)
XLA Modules:
  0.0 121.3 jit_solution(2988151225906681735)
XLA Ops:
  0.6 2.7 %shard_map.69 = bf16[32,8,384]{2,1,0:T(8,128)(2,1)} custom-call(f32[2]{0:T(128)} %fit_ref.1, bf16[16,4096]{1,0:T(8,128)(2,1)} %win_hbm.1, bf16[2,4,4096]{2,1,0:T(4,128)(2,1)} %a_hbm.3, bf16[2,4,11008]{2,1,0:T(4,128)(2,1)} %b_hbm.1), custom_call_target="tpu_custom_call" | custom-call | flops 16777216 | bytes 1048576 | tf_op jit(solution)/shard_map/pallas_call | solution.py:33
  3.3 15.4 %all-to-all-start = ((bf16[32,8,384]{2,1,0:T(8,128)(2,1)}), bf16[32,8,384]{2,1,0:T(8,128)(2,1)S(1)}, u32[]{:S(2)}, u32[]{:S(2)}) async-start(bf16[32,8,384]{2,1,0:T(8,128)(2,1)} %shard_map.69), calls=%async_computation | async-start | bytes 393216 | tf_op jit(solution)/shard_map/all_to_all | solution.py:252
  18.7 1.5 %shard_map.72 = bf16[8,8,512]{2,1,0:T(8,128)(2,1)} custom-call(bf16[2,4,4096]{2,1,0:T(4,128)(2,1)} %a_hbm.3), custom_call_target="tpu_custom_call" | custom-call | flops 1048576 | bytes 1048576 | tf_op jit(solution)/shard_map/pallas_call | solution.py:33
  20.2 16.8 %all-to-all-done.in_ref = bf16[32,8,384]{2,1,0:T(8,128)(2,1)S(1)} async-done(((bf16[32,8,384]{2,1,0:T(8,128)(2,1)}), bf16[32,8,384]{2,1,0:T(8,128)(2,1)S(1)}, u32[]{:S(2)}, u32[]{:S(2)}) %all-to-all-start) | async-done | bytes 196640 | tf_op jit(solution)/shard_map/all_to_all | solution.py:252
  37.0 5.8 %all-to-all-start.2 = ((bf16[8,8,512]{2,1,0:T(8,128)(2,1)}), bf16[8,8,512]{2,1,0:T(8,128)(2,1)S(1)}, u32[]{:S(2)}, u32[]{:S(2)}) async-start(bf16[8,8,512]{2,1,0:T(8,128)(2,1)} %shard_map.72), calls=%async_computation.2 | async-start | bytes 131072 | tf_op jit(solution)/shard_map/all_to_all | solution.py:252
  42.9 1.4 %shard_map.70 = (bf16[16,352,128]{2,1,0:T(8,128)(2,1)}, bf16[208,256]{1,0:T(8,128)(2,1)S(1)}, bf16[208,256]{1,0:T(8,128)(2,1)S(1)}) custom-call(bf16[32,8,384]{2,1,0:T(8,128)(2,1)S(1)} %all-to-all-done.in_ref), custom_call_target="tpu_custom_call" | custom-call | flops 16777216 | bytes 1048576 | tf_op jit(solution)/shard_map/pallas_call | solution.py:33
  44.2 3.7 %all-to-all-done.2 = bf16[8,8,512]{2,1,0:T(8,128)(2,1)S(1)} async-done(((bf16[8,8,512]{2,1,0:T(8,128)(2,1)}), bf16[8,8,512]{2,1,0:T(8,128)(2,1)S(1)}, u32[]{:S(2)}, u32[]{:S(2)}) %all-to-all-start.2) | async-done | bytes 65568 | tf_op jit(solution)/shard_map/all_to_all | solution.py:252
  47.9 4.8 %all-to-all-start.1 = ((bf16[16,352,128]{2,1,0:T(8,128)(2,1)}), bf16[16,352,128]{2,1,0:T(8,128)(2,1)S(1)}, u32[]{:S(2)}, u32[]{:S(2)}) async-start(bf16[16,352,128]{2,1,0:T(8,128)(2,1)} %get-tuple-element.10), calls=%async_computation.1 | async-start | bytes 2883584 | tf_op jit(solution)/shard_map/all_to_all | solution.py:252
  52.7 3.5 %collective-permute-start.1 = (bf16[1,8,8,512]{3,2,1,0:T(8,128)(2,1)S(1)}, bf16[1,8,8,512]{3,2,1,0:T(8,128)(2,1)S(1)}, u32[]{:S(2)}, u32[]{:S(2)}) collective-permute-start(bf16[1,8,8,512]{3,2,1,0:T(8,128)(2,1)S(1)} %bitcast.1), channel_id=1, source_target_pairs={{0,44},{4,48},{8,52},{12,56},{16,60},{20,0},{24,4},{28,8},{32,12},... | collective-permute-start | bytes 196616 | tf_op jit(solution)/shard_map/ppermute | solution.py:244
  56.3 7.1 %collective-permute-start.2 = (bf16[1,8,8,512]{3,2,1,0:T(8,128)(2,1)S(1)}, bf16[1,8,8,512]{3,2,1,0:T(8,128)(2,1)S(1)}, u32[]{:S(2)}, u32[]{:S(2)}) collective-permute-start(bf16[1,8,8,512]{3,2,1,0:T(8,128)(2,1)S(1)} %bitcast.2), channel_id=1, source_target_pairs={{0,20},{4,24},{8,28},{12,32},{16,36},{20,40},{24,44},{28,48},{32,5... | collective-permute-start | bytes 196616 | tf_op jit(solution)/shard_map/ppermute | solution.py:244
  63.4 4.6 %collective-permute-done.1 = bf16[1,8,8,512]{3,2,1,0:T(8,128)(2,1)S(1)} collective-permute-done((bf16[1,8,8,512]{3,2,1,0:T(8,128)(2,1)S(1)}, bf16[1,8,8,512]{3,2,1,0:T(8,128)(2,1)S(1)}, u32[]{:S(2)}, u32[]{:S(2)}) %collective-permute-start.1) | collective-permute-done | bytes 65568 | tf_op jit(solution)/shard_map/ppermute | solution.py:244
  68.0 4.4 %collective-permute-done.2 = bf16[1,8,8,512]{3,2,1,0:T(8,128)(2,1)S(1)} collective-permute-done((bf16[1,8,8,512]{3,2,1,0:T(8,128)(2,1)S(1)}, bf16[1,8,8,512]{3,2,1,0:T(8,128)(2,1)S(1)}, u32[]{:S(2)}, u32[]{:S(2)}) %collective-permute-start.2) | collective-permute-done | bytes 65568 | tf_op jit(solution)/shard_map/ppermute | solution.py:244
  72.4 1.9 %collective-permute-start.3 = (bf16[3,8,8,512]{3,2,1,0:T(8,128)(2,1)S(1)}, bf16[3,8,8,512]{3,2,1,0:T(8,128)(2,1)S(1)}, u32[]{:S(2)}, u32[]{:S(2)}) collective-permute-start(bf16[3,8,8,512]{3,2,1,0:T(8,128)(2,1)S(1)} %pad_maximum_fusion.refs_0_), channel_id=1, source_target_pairs={{0,60},{4,0},{8,4},{12,8},{16,12},{20,16},{24,20},{28,24},{32,28},... | collective-permute-start | bytes 589832 | tf_op jit(solution)/shard_map/ppermute | solution.py:244
  74.4 3.9 %collective-permute-start.4 = (bf16[3,8,8,512]{3,2,1,0:T(8,128)(2,1)S(1)}, bf16[3,8,8,512]{3,2,1,0:T(8,128)(2,1)S(1)}, u32[]{:S(2)}, u32[]{:S(2)}) collective-permute-start(bf16[3,8,8,512]{3,2,1,0:T(8,128)(2,1)S(1)} %pad_maximum_fusion.refs_0_), channel_id=1, source_target_pairs={{0,4},{4,8},{8,12},{12,16},{16,20},{20,24},{24,28},{28,32},{32,36}... | collective-permute-start | bytes 589832 | tf_op jit(solution)/shard_map/ppermute | solution.py:244
  78.3 2.8 %collective-permute-done.3.refs_1_ = bf16[3,8,8,512]{3,2,1,0:T(8,128)(2,1)S(1)} collective-permute-done((bf16[3,8,8,512]{3,2,1,0:T(8,128)(2,1)S(1)}, bf16[3,8,8,512]{3,2,1,0:T(8,128)(2,1)S(1)}, u32[]{:S(2)}, u32[]{:S(2)}) %collective-permute-start.3) | collective-permute-done | bytes 196640 | tf_op jit(solution)/shard_map/ppermute | solution.py:244
  81.1 2.2 %collective-permute-start.5 = (bf16[3,8,8,512]{3,2,1,0:T(8,128)(2,1)S(1)}, bf16[3,8,8,512]{3,2,1,0:T(8,128)(2,1)S(1)}, u32[]{:S(2)}, u32[]{:S(2)}) collective-permute-start(bf16[3,8,8,512]{3,2,1,0:T(8,128)(2,1)S(1)} %collective-permute-done.3.refs_1_), channel_id=1, source_target_pairs={{0,60},{4,0},{8,4},{12,8},{16,12},{20,16},{24,20},{28,24},{32,28},... | collective-permute-start | bytes 589832 | tf_op jit(solution)/shard_map/ppermute | solution.py:244
  83.3 0.0 collective-permute-done.4.refs_2_
  83.3 3.6 %collective-permute-start.6 = (bf16[3,8,8,512]{3,2,1,0:T(8,128)(2,1)S(1)}, bf16[3,8,8,512]{3,2,1,0:T(8,128)(2,1)S(1)}, u32[]{:S(2)}, u32[]{:S(2)}) collective-permute-start(bf16[3,8,8,512]{3,2,1,0:T(8,128)(2,1)S(1)} %collective-permute-done.4.refs_2_), channel_id=1, source_target_pairs={{0,4},{4,8},{8,12},{12,16},{16,20},{20,24},{24,28},{28,32},{32,36}... | collective-permute-start | bytes 589832 | tf_op jit(solution)/shard_map/ppermute | solution.py:244
  86.9 1.9 %collective-permute-start.7 = (bf16[1,8,8,512]{3,2,1,0:T(8,128)(2,1)S(1)}, bf16[1,8,8,512]{3,2,1,0:T(8,128)(2,1)S(1)}, u32[]{:S(2)}, u32[]{:S(2)}) collective-permute-start(bf16[1,8,8,512]{3,2,1,0:T(8,128)(2,1)S(1)} %collective-permute-done.1), channel_id=1, source_target_pairs={{0,52},{4,56},{8,60},{12,0},{16,4},{20,8},{24,12},{28,16},{32,20},... | collective-permute-start | bytes 196616 | tf_op jit(solution)/shard_map/ppermute | solution.py:244
  88.9 8.1 %collective-permute-done.7.refs_5_ = bf16[1,8,8,512]{3,2,1,0:T(8,128)(2,1)S(1)} collective-permute-done((bf16[1,8,8,512]{3,2,1,0:T(8,128)(2,1)S(1)}, bf16[1,8,8,512]{3,2,1,0:T(8,128)(2,1)S(1)}, u32[]{:S(2)}, u32[]{:S(2)}) %collective-permute-start.7) | collective-permute-done | bytes 65568 | tf_op jit(solution)/shard_map/ppermute | solution.py:244
  97.0 0.0 collective-permute-done.5.refs_3_
  97.0 0.0 collective-permute-done.6.refs_4_
  97.0 0.0 all-to-all-done.1.w_ref
  97.0 0.4 shard_map.74
  97.4 0.0 copy-start
  97.4 0.0 copy-start.1
  97.5 2.1 %collective-permute-start.9 = (f32[176,512]{1,0:T(8,128)S(1)}, f32[176,512]{1,0:T(8,128)S(1)}, u32[]{:S(2)}, u32[]{:S(2)}) collective-permute-start(f32[176,512]{1,0:T(8,128)S(1)} %shard_map.74), channel_id=1, source_target_pairs={{0,1},{1,0},{2,3},{3,2},{4,5},{5,4},{6,7},{7,6},{8,9},{9,8},{10,11... | collective-permute-start | bytes 1081352 | tf_op jit(solution)/shard_map/ppermute | solution.py:248
  99.5 0.8 shard_map.73
  100.3 2.4 %collective-permute-start.8 = (f32[176,512]{1,0:T(8,128)S(1)}, f32[176,512]{1,0:T(8,128)S(1)}, u32[]{:S(2)}, u32[]{:S(2)}) collective-permute-start(f32[176,512]{1,0:T(8,128)S(1)} %get-tuple-element.12), channel_id=1, source_target_pairs={{0,1},{1,0},{2,3},{3,2},{4,5},{5,4},{6,7},{7,6},{8,9},{9,8},{10,11... | collective-permute-start | bytes 1081352 | tf_op jit(solution)/shard_map/ppermute | solution.py:248
  102.7 0.0 collective-permute-done.9
  102.8 0.1 add.10
  102.8 4.8 %collective-permute-start.10 = (f32[176,512]{1,0:T(8,128)S(1)}, f32[176,512]{1,0:T(8,128)S(1)}, u32[]{:S(2)}, u32[]{:S(2)}) collective-permute-start(f32[176,512]{1,0:T(8,128)S(1)} %add.10), channel_id=1, source_target_pairs={{0,2},{2,0},{1,3},{3,1},{4,6},{6,4},{5,7},{7,5},{8,10},{10,8},{9,1... | collective-permute-start | bytes 1081352 | tf_op jit(solution)/shard_map/ppermute | solution.py:248
  107.6 2.5 %collective-permute-start = (bf16[208,256]{1,0:T(8,128)(2,1)S(1)}, bf16[208,256]{1,0:T(8,128)(2,1)S(1)}, u32[]{:S(2)}, u32[]{:S(2)}) collective-permute-start(bf16[208,256]{1,0:T(8,128)(2,1)S(1)} %get-tuple-element.9), channel_id=1, source_target_pairs={{0,2},{2,0},{1,3},{3,1},{4,6},{6,4},{5,7},{7,5},{8,10},{10,8},{9,1... | collective-permute-start | bytes 319496 | tf_op jit(solution)/shard_map/ppermute | solution.py:248
  110.2 0.0 copy-done
  110.2 0.0 copy-done.1
  110.2 0.5 shard_map.68.base_ref
  110.7 8.1 %collective-permute-done.got_ref = bf16[208,256]{1,0:T(8,128)(2,1)S(1)} collective-permute-done((bf16[208,256]{1,0:T(8,128)(2,1)S(1)}, bf16[208,256]{1,0:T(8,128)(2,1)S(1)}, u32[]{:S(2)}, u32[]{:S(2)}) %collective-permute-start) | collective-permute-done | bytes 106528 | tf_op jit(solution)/shard_map/ppermute | solution.py:248
  118.8 1.6 %shard_map.71 = bf16[172,2048]{1,0:T(8,128)(2,1)} custom-call(f32[172,128]{1,0:T(8,128)S(1)} %shard_map.68.base_ref, bf16[208,256]{1,0:T(8,128)(2,1)S(1)} %get-tuple-element.8.keep_ref, bf16[208,256]{1,0:T(8,128)(2,1)S(1)} %collective-permute-done.got_ref), custom_call_target="tpu_custom_call" | custom-call | flops 1073741824 | bytes 1048576 | tf_op jit(solution)/shard_map/pallas_call | solution.py:33
  120.5 0.0 collective-permute-done.8
  120.5 0.0 collective-permute-done.10
  120.5 0.8 fusion
  (1 shorter events, 0.0 us)
Async XLA Ops:
  3.3 33.7 %all-to-all-start = ((bf16[32,8,384]{2,1,0:T(8,128)(2,1)}), bf16[32,8,384]{2,1,0:T(8,128)(2,1)S(1)}, u32[]{:S(2)}, u32[]{:S(2)}) async-start(bf16[32,8,384]{2,1,0:T(8,128)(2,1)} %shard_map.69), calls=%async_computation | async-start | bytes 393216 | tf_op jit(solution)/shard_map/all_to_all | solution.py:252
  37.0 10.9 %all-to-all-start.2 = ((bf16[8,8,512]{2,1,0:T(8,128)(2,1)}), bf16[8,8,512]{2,1,0:T(8,128)(2,1)S(1)}, u32[]{:S(2)}, u32[]{:S(2)}) async-start(bf16[8,8,512]{2,1,0:T(8,128)(2,1)} %shard_map.72), calls=%async_computation.2 | async-start | bytes 131072 | tf_op jit(solution)/shard_map/all_to_all | solution.py:252
  47.9 49.0 %all-to-all-start.1 = ((bf16[16,352,128]{2,1,0:T(8,128)(2,1)}), bf16[16,352,128]{2,1,0:T(8,128)(2,1)S(1)}, u32[]{:S(2)}, u32[]{:S(2)}) async-start(bf16[16,352,128]{2,1,0:T(8,128)(2,1)} %get-tuple-element.10), calls=%async_computation.1 | async-start | bytes 2883584 | tf_op jit(solution)/shard_map/all_to_all | solution.py:252
  52.7 15.3 %collective-permute-start.1 = (bf16[1,8,8,512]{3,2,1,0:T(8,128)(2,1)S(1)}, bf16[1,8,8,512]{3,2,1,0:T(8,128)(2,1)S(1)}, u32[]{:S(2)}, u32[]{:S(2)}) collective-permute-start(bf16[1,8,8,512]{3,2,1,0:T(8,128)(2,1)S(1)} %bitcast.1), channel_id=1, source_target_pairs={{0,44},{4,48},{8,52},{12,56},{16,60},{20,0},{24,4},{28,8},{32,12},... | collective-permute-start | bytes 196616 | tf_op jit(solution)/shard_map/ppermute | solution.py:244
  56.3 16.2 %collective-permute-start.2 = (bf16[1,8,8,512]{3,2,1,0:T(8,128)(2,1)S(1)}, bf16[1,8,8,512]{3,2,1,0:T(8,128)(2,1)S(1)}, u32[]{:S(2)}, u32[]{:S(2)}) collective-permute-start(bf16[1,8,8,512]{3,2,1,0:T(8,128)(2,1)S(1)} %bitcast.2), channel_id=1, source_target_pairs={{0,20},{4,24},{8,28},{12,32},{16,36},{20,40},{24,44},{28,48},{32,5... | collective-permute-start | bytes 196616 | tf_op jit(solution)/shard_map/ppermute | solution.py:244
  72.4 8.7 %collective-permute-start.3 = (bf16[3,8,8,512]{3,2,1,0:T(8,128)(2,1)S(1)}, bf16[3,8,8,512]{3,2,1,0:T(8,128)(2,1)S(1)}, u32[]{:S(2)}, u32[]{:S(2)}) collective-permute-start(bf16[3,8,8,512]{3,2,1,0:T(8,128)(2,1)S(1)} %pad_maximum_fusion.refs_0_), channel_id=1, source_target_pairs={{0,60},{4,0},{8,4},{12,8},{16,12},{20,16},{24,20},{28,24},{32,28},... | collective-permute-start | bytes 589832 | tf_op jit(solution)/shard_map/ppermute | solution.py:244
  74.4 8.9 %collective-permute-start.4 = (bf16[3,8,8,512]{3,2,1,0:T(8,128)(2,1)S(1)}, bf16[3,8,8,512]{3,2,1,0:T(8,128)(2,1)S(1)}, u32[]{:S(2)}, u32[]{:S(2)}) collective-permute-start(bf16[3,8,8,512]{3,2,1,0:T(8,128)(2,1)S(1)} %pad_maximum_fusion.refs_0_), channel_id=1, source_target_pairs={{0,4},{4,8},{8,12},{12,16},{16,20},{20,24},{24,28},{28,32},{32,36}... | collective-permute-start | bytes 589832 | tf_op jit(solution)/shard_map/ppermute | solution.py:244
  81.1 15.9 %collective-permute-start.5 = (bf16[3,8,8,512]{3,2,1,0:T(8,128)(2,1)S(1)}, bf16[3,8,8,512]{3,2,1,0:T(8,128)(2,1)S(1)}, u32[]{:S(2)}, u32[]{:S(2)}) collective-permute-start(bf16[3,8,8,512]{3,2,1,0:T(8,128)(2,1)S(1)} %collective-permute-done.3.refs_1_), channel_id=1, source_target_pairs={{0,60},{4,0},{8,4},{12,8},{16,12},{20,16},{24,20},{28,24},{32,28},... | collective-permute-start | bytes 589832 | tf_op jit(solution)/shard_map/ppermute | solution.py:244
  83.3 13.7 %collective-permute-start.6 = (bf16[3,8,8,512]{3,2,1,0:T(8,128)(2,1)S(1)}, bf16[3,8,8,512]{3,2,1,0:T(8,128)(2,1)S(1)}, u32[]{:S(2)}, u32[]{:S(2)}) collective-permute-start(bf16[3,8,8,512]{3,2,1,0:T(8,128)(2,1)S(1)} %collective-permute-done.4.refs_2_), channel_id=1, source_target_pairs={{0,4},{4,8},{8,12},{12,16},{16,20},{20,24},{24,28},{28,32},{32,36}... | collective-permute-start | bytes 589832 | tf_op jit(solution)/shard_map/ppermute | solution.py:244
  86.9 10.0 %collective-permute-start.7 = (bf16[1,8,8,512]{3,2,1,0:T(8,128)(2,1)S(1)}, bf16[1,8,8,512]{3,2,1,0:T(8,128)(2,1)S(1)}, u32[]{:S(2)}, u32[]{:S(2)}) collective-permute-start(bf16[1,8,8,512]{3,2,1,0:T(8,128)(2,1)S(1)} %collective-permute-done.1), channel_id=1, source_target_pairs={{0,52},{4,56},{8,60},{12,0},{16,4},{20,8},{24,12},{28,16},{32,20},... | collective-permute-start | bytes 196616 | tf_op jit(solution)/shard_map/ppermute | solution.py:244
  97.4 12.8 %copy-start = (bf16[172,4096]{1,0:T(8,128)(2,1)S(1)}, bf16[172,4096]{1,0:T(8,128)(2,1)}, u32[]{:S(2)}) copy-start(bf16[172,4096]{1,0:T(8,128)(2,1)} %weight_ref.1) | copy-start | bytes 4227076
  97.4 12.7 %copy-start.1 = (bf16[16,4096]{1,0:T(8,128)(2,1)S(1)}, bf16[16,4096]{1,0:T(8,128)(2,1)}, u32[]{:S(2)}) copy-start(bf16[16,4096]{1,0:T(8,128)(2,1)} %win_hbm.1) | copy-start | bytes 393220
  97.5 5.3 %collective-permute-start.9 = (f32[176,512]{1,0:T(8,128)S(1)}, f32[176,512]{1,0:T(8,128)S(1)}, u32[]{:S(2)}, u32[]{:S(2)}) collective-permute-start(f32[176,512]{1,0:T(8,128)S(1)} %shard_map.74), channel_id=1, source_target_pairs={{0,1},{1,0},{2,3},{3,2},{4,5},{5,4},{6,7},{7,6},{8,9},{9,8},{10,11... | collective-permute-start | bytes 1081352 | tf_op jit(solution)/shard_map/ppermute | solution.py:248
  100.3 20.1 %collective-permute-start.8 = (f32[176,512]{1,0:T(8,128)S(1)}, f32[176,512]{1,0:T(8,128)S(1)}, u32[]{:S(2)}, u32[]{:S(2)}) collective-permute-start(f32[176,512]{1,0:T(8,128)S(1)} %get-tuple-element.12), channel_id=1, source_target_pairs={{0,1},{1,0},{2,3},{3,2},{4,5},{5,4},{6,7},{7,6},{8,9},{9,8},{10,11... | collective-permute-start | bytes 1081352 | tf_op jit(solution)/shard_map/ppermute | solution.py:248
  102.8 17.7 %collective-permute-start.10 = (f32[176,512]{1,0:T(8,128)S(1)}, f32[176,512]{1,0:T(8,128)S(1)}, u32[]{:S(2)}, u32[]{:S(2)}) collective-permute-start(f32[176,512]{1,0:T(8,128)S(1)} %add.10), channel_id=1, source_target_pairs={{0,2},{2,0},{1,3},{3,1},{4,6},{6,4},{5,7},{7,5},{8,10},{10,8},{9,1... | collective-permute-start | bytes 1081352 | tf_op jit(solution)/shard_map/ppermute | solution.py:248
  107.6 11.2 %collective-permute-start = (bf16[208,256]{1,0:T(8,128)(2,1)S(1)}, bf16[208,256]{1,0:T(8,128)(2,1)S(1)}, u32[]{:S(2)}, u32[]{:S(2)}) collective-permute-start(bf16[208,256]{1,0:T(8,128)(2,1)S(1)} %get-tuple-element.9), channel_id=1, source_target_pairs={{0,2},{2,0},{1,3},{3,1},{4,6},{6,4},{5,7},{7,5},{8,10},{10,8},{9,1... | collective-permute-start | bytes 319496 | tf_op jit(solution)/shard_map/ppermute | solution.py:248

commit v4 on v3

--- a/solution.py
+++ b/solution.py
@@ -205,7 +205,7 @@
     z = lax.axis_index("z")
     for ref, offsets in zip(chunks, OFFSETS):
         for i, offset in enumerate(offsets):
-            place = lax.rem(z + offset + nz, nz)
+            place = lax.rem(z + (1 - 2 * lax.axis_index("core")) * offset + nz, nz)
             for g in range(groups):
                 rows_ref[g, place] = ref[i, g]
 
@@ -241,7 +241,11 @@
 
 def shifted(value, offset):
     n = lax.axis_size("z")
-    return lax.ppermute(value, "z", [(i, (i - offset) % n) for i in range(n)])
+    pairs = []
+    for z in range(n):
+        pairs.append((2 * z, 2 * ((z - offset) % n)))
+        pairs.append((2 * z + 1, 2 * ((z + offset) % n) + 1))
+    return lax.ppermute(value, ("z", "core"), pairs)
 
 
 def swapped(value, axis):

time: 122 us -> 120 us (0.984)
  waiting for transfers between devices: 48.6 us -> 46.5 us
    ppermute x7, waiting for transfers between devices: 19.9 us -> 17.9 us  [shifted(): return lax.ppermute(value, ('z', 'core'), pairs)]
where the time goes in v4:
time: 120 us; the launch traced here: 119 us
  starting transfers between devices  62 us (52%)
  waiting for transfers between devices  46.5 us (39%)
  Pallas kernels  9.01 us (8%)
    all_to_all x3, starting transfers between devices, exchanged(): return lax.all_to_all(value, axis, 0, 0, tiled=True)  26 us
    ppermute x7, starting transfers between devices, shifted(): return lax.ppermute(value, ('z', 'core'), pairs)  24.2 us
    all_to_all x3, waiting for transfers between devices, exchanged(): return lax.all_to_all(value, axis, 0, 0, tiled=True)  20.5 us
    ppermute x7, waiting for transfers between devices, shifted(): return lax.ppermute(value, ('z', 'core'), pairs)  17.9 us
    ppermute x4, starting transfers between devices, swapped(): return lax.ppermute(value, axis, [(0, 1), (1, 0)])  11.8 us
    pallas_call x7, Pallas kernels, call(): pl.pallas_call(body, out_shape=out_shape, in_specs=[scalar if i in smem e...  9.01 us
    ppermute x4, waiting for transfers between devices, swapped(): return lax.ppermute(value, axis, [(0, 1), (1, 0)])  8.1 us
  transfers between devices with their start and end apart: 14, of which 7 were waited for; matrix products, arithmetic and copies ran while one was open for 0% of the time, Pallas kernels for 5%

profile of v4, /device:TPU:34, one launch (start us, length us, event | category | flops | bytes accessed | tf_op | source)
XLA Modules:
  0.0 119.3 jit_solution(1281098800889660043)
XLA Ops:
  0.6 2.7 %shard_map.69 = bf16[32,8,384]{2,1,0:T(8,128)(2,1)} custom-call(f32[2]{0:T(128)} %fit_ref.1, bf16[16,4096]{1,0:T(8,128)(2,1)} %win_hbm.1, bf16[2,4,4096]{2,1,0:T(4,128)(2,1)} %a_hbm.3, bf16[2,4,11008]{2,1,0:T(4,128)(2,1)} %b_hbm.1), custom_call_target="tpu_custom_call" | custom-call | flops 16777216 | bytes 1048576 | tf_op jit(solution)/shard_map/pallas_call | solution.py:33
  3.3 15.4 %all-to-all-start = ((bf16[32,8,384]{2,1,0:T(8,128)(2,1)}), bf16[32,8,384]{2,1,0:T(8,128)(2,1)S(1)}, u32[]{:S(2)}, u32[]{:S(2)}) async-start(bf16[32,8,384]{2,1,0:T(8,128)(2,1)} %shard_map.69), calls=%async_computation | async-start | bytes 393216 | tf_op jit(solution)/shard_map/all_to_all | solution.py:256
  18.7 1.5 %shard_map.72 = bf16[8,8,512]{2,1,0:T(8,128)(2,1)} custom-call(bf16[2,4,4096]{2,1,0:T(4,128)(2,1)} %a_hbm.3), custom_call_target="tpu_custom_call" | custom-call | flops 1048576 | bytes 1048576 | tf_op jit(solution)/shard_map/pallas_call | solution.py:33
  20.2 16.8 %all-to-all-done.in_ref = bf16[32,8,384]{2,1,0:T(8,128)(2,1)S(1)} async-done(((bf16[32,8,384]{2,1,0:T(8,128)(2,1)}), bf16[32,8,384]{2,1,0:T(8,128)(2,1)S(1)}, u32[]{:S(2)}, u32[]{:S(2)}) %all-to-all-start) | async-done | bytes 196640 | tf_op jit(solution)/shard_map/all_to_all | solution.py:256
  37.0 5.8 %all-to-all-start.2 = ((bf16[8,8,512]{2,1,0:T(8,128)(2,1)}), bf16[8,8,512]{2,1,0:T(8,128)(2,1)S(1)}, u32[]{:S(2)}, u32[]{:S(2)}) async-start(bf16[8,8,512]{2,1,0:T(8,128)(2,1)} %shard_map.72), calls=%async_computation.2 | async-start | bytes 131072 | tf_op jit(solution)/shard_map/all_to_all | solution.py:256
  42.9 1.4 %shard_map.70 = (bf16[16,352,128]{2,1,0:T(8,128)(2,1)}, bf16[208,256]{1,0:T(8,128)(2,1)S(1)}, bf16[208,256]{1,0:T(8,128)(2,1)S(1)}) custom-call(bf16[32,8,384]{2,1,0:T(8,128)(2,1)S(1)} %all-to-all-done.in_ref), custom_call_target="tpu_custom_call" | custom-call | flops 16777216 | bytes 1048576 | tf_op jit(solution)/shard_map/pallas_call | solution.py:33
  44.2 3.7 %all-to-all-done.2 = bf16[8,8,512]{2,1,0:T(8,128)(2,1)S(1)} async-done(((bf16[8,8,512]{2,1,0:T(8,128)(2,1)}), bf16[8,8,512]{2,1,0:T(8,128)(2,1)S(1)}, u32[]{:S(2)}, u32[]{:S(2)}) %all-to-all-start.2) | async-done | bytes 65568 | tf_op jit(solution)/shard_map/all_to_all | solution.py:256
  47.9 4.8 %all-to-all-start.1 = ((bf16[16,352,128]{2,1,0:T(8,128)(2,1)}), bf16[16,352,128]{2,1,0:T(8,128)(2,1)S(1)}, u32[]{:S(2)}, u32[]{:S(2)}) async-start(bf16[16,352,128]{2,1,0:T(8,128)(2,1)} %get-tuple-element.10), calls=%async_computation.1 | async-start | bytes 2883584 | tf_op jit(solution)/shard_map/all_to_all | solution.py:256
  52.7 3.5 %collective-permute-start.1 = (bf16[1,8,8,512]{3,2,1,0:T(8,128)(2,1)S(1)}, bf16[1,8,8,512]{3,2,1,0:T(8,128)(2,1)S(1)}, u32[]{:S(2)}, u32[]{:S(2)}) collective-permute-start(bf16[1,8,8,512]{3,2,1,0:T(8,128)(2,1)S(1)} %bitcast.1), channel_id=1, source_target_pairs={{0,44},{1,21},{4,48},{5,25},{8,52},{9,29},{12,56},{13,33},{16,60},... | collective-permute-start | bytes 196616 | tf_op jit(solution)/shard_map/ppermute | solution.py:248
  56.3 7.1 %collective-permute-start.2 = (bf16[1,8,8,512]{3,2,1,0:T(8,128)(2,1)S(1)}, bf16[1,8,8,512]{3,2,1,0:T(8,128)(2,1)S(1)}, u32[]{:S(2)}, u32[]{:S(2)}) collective-permute-start(bf16[1,8,8,512]{3,2,1,0:T(8,128)(2,1)S(1)} %bitcast.2), channel_id=1, source_target_pairs={{0,20},{1,45},{4,24},{5,49},{8,28},{9,53},{12,32},{13,57},{16,36},... | collective-permute-start | bytes 196616 | tf_op jit(solution)/shard_map/ppermute | solution.py:248
  63.4 0.9 collective-permute-done.1
  64.3 5.8 %collective-permute-done.2 = bf16[1,8,8,512]{3,2,1,0:T(8,128)(2,1)S(1)} collective-permute-done((bf16[1,8,8,512]{3,2,1,0:T(8,128)(2,1)S(1)}, bf16[1,8,8,512]{3,2,1,0:T(8,128)(2,1)S(1)}, u32[]{:S(2)}, u32[]{:S(2)}) %collective-permute-start.2) | collective-permute-done | bytes 65568 | tf_op jit(solution)/shard_map/ppermute | solution.py:248
  70.1 2.1 %collective-permute-start.3 = (bf16[3,8,8,512]{3,2,1,0:T(8,128)(2,1)S(1)}, bf16[3,8,8,512]{3,2,1,0:T(8,128)(2,1)S(1)}, u32[]{:S(2)}, u32[]{:S(2)}) collective-permute-start(bf16[3,8,8,512]{3,2,1,0:T(8,128)(2,1)S(1)} %pad_maximum_fusion.refs_0_), channel_id=1, source_target_pairs={{0,60},{1,5},{4,0},{5,9},{8,4},{9,13},{12,8},{13,17},{16,12},{17,2... | collective-permute-start | bytes 589832 | tf_op jit(solution)/shard_map/ppermute | solution.py:248
  72.1 3.8 %collective-permute-start.4 = (bf16[3,8,8,512]{3,2,1,0:T(8,128)(2,1)S(1)}, bf16[3,8,8,512]{3,2,1,0:T(8,128)(2,1)S(1)}, u32[]{:S(2)}, u32[]{:S(2)}) collective-permute-start(bf16[3,8,8,512]{3,2,1,0:T(8,128)(2,1)S(1)} %pad_maximum_fusion.refs_0_), channel_id=1, source_target_pairs={{0,4},{1,61},{4,8},{5,1},{8,12},{9,5},{12,16},{13,9},{16,20},{17,1... | collective-permute-start | bytes 589832 | tf_op jit(solution)/shard_map/ppermute | solution.py:248
  75.9 3.8 %collective-permute-done.3.refs_1_ = bf16[3,8,8,512]{3,2,1,0:T(8,128)(2,1)S(1)} collective-permute-done((bf16[3,8,8,512]{3,2,1,0:T(8,128)(2,1)S(1)}, bf16[3,8,8,512]{3,2,1,0:T(8,128)(2,1)S(1)}, u32[]{:S(2)}, u32[]{:S(2)}) %collective-permute-start.3) | collective-permute-done | bytes 196640 | tf_op jit(solution)/shard_map/ppermute | solution.py:248
  79.7 1.9 %collective-permute-start.5 = (bf16[3,8,8,512]{3,2,1,0:T(8,128)(2,1)S(1)}, bf16[3,8,8,512]{3,2,1,0:T(8,128)(2,1)S(1)}, u32[]{:S(2)}, u32[]{:S(2)}) collective-permute-start(bf16[3,8,8,512]{3,2,1,0:T(8,128)(2,1)S(1)} %collective-permute-done.3.refs_1_), channel_id=1, source_target_pairs={{0,60},{1,5},{4,0},{5,9},{8,4},{9,13},{12,8},{13,17},{16,12},{17,2... | collective-permute-start | bytes 589832 | tf_op jit(solution)/shard_map/ppermute | solution.py:248
  81.6 0.0 collective-permute-done.4.refs_2_
  81.6 3.9 %collective-permute-start.6 = (bf16[3,8,8,512]{3,2,1,0:T(8,128)(2,1)S(1)}, bf16[3,8,8,512]{3,2,1,0:T(8,128)(2,1)S(1)}, u32[]{:S(2)}, u32[]{:S(2)}) collective-permute-start(bf16[3,8,8,512]{3,2,1,0:T(8,128)(2,1)S(1)} %collective-permute-done.4.refs_2_), channel_id=1, source_target_pairs={{0,4},{1,61},{4,8},{5,1},{8,12},{9,5},{12,16},{13,9},{16,20},{17,1... | collective-permute-start | bytes 589832 | tf_op jit(solution)/shard_map/ppermute | solution.py:248
  85.6 1.9 %collective-permute-start.7 = (bf16[1,8,8,512]{3,2,1,0:T(8,128)(2,1)S(1)}, bf16[1,8,8,512]{3,2,1,0:T(8,128)(2,1)S(1)}, u32[]{:S(2)}, u32[]{:S(2)}) collective-permute-start(bf16[1,8,8,512]{3,2,1,0:T(8,128)(2,1)S(1)} %collective-permute-done.1), channel_id=1, source_target_pairs={{0,52},{1,13},{4,56},{5,17},{8,60},{9,21},{12,0},{13,25},{16,4},{1... | collective-permute-start | bytes 196616 | tf_op jit(solution)/shard_map/ppermute | solution.py:248
  87.5 7.4 %collective-permute-done.7.refs_5_ = bf16[1,8,8,512]{3,2,1,0:T(8,128)(2,1)S(1)} collective-permute-done((bf16[1,8,8,512]{3,2,1,0:T(8,128)(2,1)S(1)}, bf16[1,8,8,512]{3,2,1,0:T(8,128)(2,1)S(1)}, u32[]{:S(2)}, u32[]{:S(2)}) %collective-permute-start.7) | collective-permute-done | bytes 65568 | tf_op jit(solution)/shard_map/ppermute | solution.py:248
  94.9 0.0 collective-permute-done.5.refs_3_
  94.9 0.0 collective-permute-done.6.refs_4_
  94.9 0.0 all-to-all-done.1.w_ref
  94.9 0.5 shard_map.74
  95.4 0.0 copy-start
  95.4 0.0 copy-start.1
  95.4 2.1 %collective-permute-start.9 = (f32[176,512]{1,0:T(8,128)S(1)}, f32[176,512]{1,0:T(8,128)S(1)}, u32[]{:S(2)}, u32[]{:S(2)}) collective-permute-start(f32[176,512]{1,0:T(8,128)S(1)} %shard_map.74), channel_id=1, source_target_pairs={{0,1},{1,0},{2,3},{3,2},{4,5},{5,4},{6,7},{7,6},{8,9},{9,8},{10,11... | collective-permute-start | bytes 1081352 | tf_op jit(solution)/shard_map/ppermute | solution.py:252
  97.5 0.8 shard_map.73
  98.3 2.4 %collective-permute-start.8 = (f32[176,512]{1,0:T(8,128)S(1)}, f32[176,512]{1,0:T(8,128)S(1)}, u32[]{:S(2)}, u32[]{:S(2)}) collective-permute-start(f32[176,512]{1,0:T(8,128)S(1)} %get-tuple-element.12), channel_id=1, source_target_pairs={{0,1},{1,0},{2,3},{3,2},{4,5},{5,4},{6,7},{7,6},{8,9},{9,8},{10,11... | collective-permute-start | bytes 1081352 | tf_op jit(solution)/shard_map/ppermute | solution.py:252
  100.7 0.0 collective-permute-done.9
  100.7 0.1 add.10
  100.8 4.8 %collective-permute-start.10 = (f32[176,512]{1,0:T(8,128)S(1)}, f32[176,512]{1,0:T(8,128)S(1)}, u32[]{:S(2)}, u32[]{:S(2)}) collective-permute-start(f32[176,512]{1,0:T(8,128)S(1)} %add.10), channel_id=1, source_target_pairs={{0,2},{2,0},{1,3},{3,1},{4,6},{6,4},{5,7},{7,5},{8,10},{10,8},{9,1... | collective-permute-start | bytes 1081352 | tf_op jit(solution)/shard_map/ppermute | solution.py:252
  105.6 2.5 %collective-permute-start = (bf16[208,256]{1,0:T(8,128)(2,1)S(1)}, bf16[208,256]{1,0:T(8,128)(2,1)S(1)}, u32[]{:S(2)}, u32[]{:S(2)}) collective-permute-start(bf16[208,256]{1,0:T(8,128)(2,1)S(1)} %get-tuple-element.9), channel_id=1, source_target_pairs={{0,2},{2,0},{1,3},{3,1},{4,6},{6,4},{5,7},{7,5},{8,10},{10,8},{9,1... | collective-permute-start | bytes 319496 | tf_op jit(solution)/shard_map/ppermute | solution.py:252
  108.1 0.0 copy-done
  108.1 0.0 copy-done.1
  108.1 0.5 shard_map.68.base_ref
  108.7 8.1 %collective-permute-done.got_ref = bf16[208,256]{1,0:T(8,128)(2,1)S(1)} collective-permute-done((bf16[208,256]{1,0:T(8,128)(2,1)S(1)}, bf16[208,256]{1,0:T(8,128)(2,1)S(1)}, u32[]{:S(2)}, u32[]{:S(2)}) %collective-permute-start) | collective-permute-done | bytes 106528 | tf_op jit(solution)/shard_map/ppermute | solution.py:252
  116.8 1.6 %shard_map.71 = bf16[172,2048]{1,0:T(8,128)(2,1)} custom-call(f32[172,128]{1,0:T(8,128)S(1)} %shard_map.68.base_ref, bf16[208,256]{1,0:T(8,128)(2,1)S(1)} %get-tuple-element.8.keep_ref, bf16[208,256]{1,0:T(8,128)(2,1)S(1)} %collective-permute-done.got_ref), custom_call_target="tpu_custom_call" | custom-call | flops 1073741824 | bytes 1048576 | tf_op jit(solution)/shard_map/pallas_call | solution.py:33
  118.4 0.0 collective-permute-done.8
  118.4 0.0 collective-permute-done.10
  118.4 0.8 fusion
  (1 shorter events, 0.0 us)
Async XLA Ops:
  3.3 33.7 %all-to-all-start = ((bf16[32,8,384]{2,1,0:T(8,128)(2,1)}), bf16[32,8,384]{2,1,0:T(8,128)(2,1)S(1)}, u32[]{:S(2)}, u32[]{:S(2)}) async-start(bf16[32,8,384]{2,1,0:T(8,128)(2,1)} %shard_map.69), calls=%async_computation | async-start | bytes 393216 | tf_op jit(solution)/shard_map/all_to_all | solution.py:256
  37.0 10.9 %all-to-all-start.2 = ((bf16[8,8,512]{2,1,0:T(8,128)(2,1)}), bf16[8,8,512]{2,1,0:T(8,128)(2,1)S(1)}, u32[]{:S(2)}, u32[]{:S(2)}) async-start(bf16[8,8,512]{2,1,0:T(8,128)(2,1)} %shard_map.72), calls=%async_computation.2 | async-start | bytes 131072 | tf_op jit(solution)/shard_map/all_to_all | solution.py:256
  47.9 47.0 %all-to-all-start.1 = ((bf16[16,352,128]{2,1,0:T(8,128)(2,1)}), bf16[16,352,128]{2,1,0:T(8,128)(2,1)S(1)}, u32[]{:S(2)}, u32[]{:S(2)}) async-start(bf16[16,352,128]{2,1,0:T(8,128)(2,1)} %get-tuple-element.10), calls=%async_computation.1 | async-start | bytes 2883584 | tf_op jit(solution)/shard_map/all_to_all | solution.py:256
  52.7 11.6 %collective-permute-start.1 = (bf16[1,8,8,512]{3,2,1,0:T(8,128)(2,1)S(1)}, bf16[1,8,8,512]{3,2,1,0:T(8,128)(2,1)S(1)}, u32[]{:S(2)}, u32[]{:S(2)}) collective-permute-start(bf16[1,8,8,512]{3,2,1,0:T(8,128)(2,1)S(1)} %bitcast.1), channel_id=1, source_target_pairs={{0,44},{1,21},{4,48},{5,25},{8,52},{9,29},{12,56},{13,33},{16,60},... | collective-permute-start | bytes 196616 | tf_op jit(solution)/shard_map/ppermute | solution.py:248
  56.3 13.8 %collective-permute-start.2 = (bf16[1,8,8,512]{3,2,1,0:T(8,128)(2,1)S(1)}, bf16[1,8,8,512]{3,2,1,0:T(8,128)(2,1)S(1)}, u32[]{:S(2)}, u32[]{:S(2)}) collective-permute-start(bf16[1,8,8,512]{3,2,1,0:T(8,128)(2,1)S(1)} %bitcast.2), channel_id=1, source_target_pairs={{0,20},{1,45},{4,24},{5,49},{8,28},{9,53},{12,32},{13,57},{16,36},... | collective-permute-start | bytes 196616 | tf_op jit(solution)/shard_map/ppermute | solution.py:248
  70.1 9.7 %collective-permute-start.3 = (bf16[3,8,8,512]{3,2,1,0:T(8,128)(2,1)S(1)}, bf16[3,8,8,512]{3,2,1,0:T(8,128)(2,1)S(1)}, u32[]{:S(2)}, u32[]{:S(2)}) collective-permute-start(bf16[3,8,8,512]{3,2,1,0:T(8,128)(2,1)S(1)} %pad_maximum_fusion.refs_0_), channel_id=1, source_target_pairs={{0,60},{1,5},{4,0},{5,9},{8,4},{9,13},{12,8},{13,17},{16,12},{17,2... | collective-permute-start | bytes 589832 | tf_op jit(solution)/shard_map/ppermute | solution.py:248
  72.1 9.5 %collective-permute-start.4 = (bf16[3,8,8,512]{3,2,1,0:T(8,128)(2,1)S(1)}, bf16[3,8,8,512]{3,2,1,0:T(8,128)(2,1)S(1)}, u32[]{:S(2)}, u32[]{:S(2)}) collective-permute-start(bf16[3,8,8,512]{3,2,1,0:T(8,128)(2,1)S(1)} %pad_maximum_fusion.refs_0_), channel_id=1, source_target_pairs={{0,4},{1,61},{4,8},{5,1},{8,12},{9,5},{12,16},{13,9},{16,20},{17,1... | collective-permute-start | bytes 589832 | tf_op jit(solution)/shard_map/ppermute | solution.py:248
  79.7 15.2 %collective-permute-start.5 = (bf16[3,8,8,512]{3,2,1,0:T(8,128)(2,1)S(1)}, bf16[3,8,8,512]{3,2,1,0:T(8,128)(2,1)S(1)}, u32[]{:S(2)}, u32[]{:S(2)}) collective-permute-start(bf16[3,8,8,512]{3,2,1,0:T(8,128)(2,1)S(1)} %collective-permute-done.3.refs_1_), channel_id=1, source_target_pairs={{0,60},{1,5},{4,0},{5,9},{8,4},{9,13},{12,8},{13,17},{16,12},{17,2... | collective-permute-start | bytes 589832 | tf_op jit(solution)/shard_map/ppermute | solution.py:248
  81.6 13.3 %collective-permute-start.6 = (bf16[3,8,8,512]{3,2,1,0:T(8,128)(2,1)S(1)}, bf16[3,8,8,512]{3,2,1,0:T(8,128)(2,1)S(1)}, u32[]{:S(2)}, u32[]{:S(2)}) collective-permute-start(bf16[3,8,8,512]{3,2,1,0:T(8,128)(2,1)S(1)} %collective-permute-done.4.refs_2_), channel_id=1, source_target_pairs={{0,4},{1,61},{4,8},{5,1},{8,12},{9,5},{12,16},{13,9},{16,20},{17,1... | collective-permute-start | bytes 589832 | tf_op jit(solution)/shard_map/ppermute | solution.py:248
  85.6 9.3 %collective-permute-start.7 = (bf16[1,8,8,512]{3,2,1,0:T(8,128)(2,1)S(1)}, bf16[1,8,8,512]{3,2,1,0:T(8,128)(2,1)S(1)}, u32[]{:S(2)}, u32[]{:S(2)}) collective-permute-start(bf16[1,8,8,512]{3,2,1,0:T(8,128)(2,1)S(1)} %collective-permute-done.1), channel_id=1, source_target_pairs={{0,52},{1,13},{4,56},{5,17},{8,60},{9,21},{12,0},{13,25},{16,4},{1... | collective-permute-start | bytes 196616 | tf_op jit(solution)/shard_map/ppermute | solution.py:248
  95.4 12.8 %copy-start = (bf16[172,4096]{1,0:T(8,128)(2,1)S(1)}, bf16[172,4096]{1,0:T(8,128)(2,1)}, u32[]{:S(2)}) copy-start(bf16[172,4096]{1,0:T(8,128)(2,1)} %weight_ref.1) | copy-start | bytes 4227076
  95.4 12.8 %copy-start.1 = (bf16[16,4096]{1,0:T(8,128)(2,1)S(1)}, bf16[16,4096]{1,0:T(8,128)(2,1)}, u32[]{:S(2)}) copy-start(bf16[16,4096]{1,0:T(8,128)(2,1)} %win_hbm.1) | copy-start | bytes 393220
  95.4 5.3 %collective-permute-start.9 = (f32[176,512]{1,0:T(8,128)S(1)}, f32[176,512]{1,0:T(8,128)S(1)}, u32[]{:S(2)}, u32[]{:S(2)}) collective-permute-start(f32[176,512]{1,0:T(8,128)S(1)} %shard_map.74), channel_id=1, source_target_pairs={{0,1},{1,0},{2,3},{3,2},{4,5},{5,4},{6,7},{7,6},{8,9},{9,8},{10,11... | collective-permute-start | bytes 1081352 | tf_op jit(solution)/shard_map/ppermute | solution.py:252
  98.3 20.1 %collective-permute-start.8 = (f32[176,512]{1,0:T(8,128)S(1)}, f32[176,512]{1,0:T(8,128)S(1)}, u32[]{:S(2)}, u32[]{:S(2)}) collective-permute-start(f32[176,512]{1,0:T(8,128)S(1)} %get-tuple-element.12), channel_id=1, source_target_pairs={{0,1},{1,0},{2,3},{3,2},{4,5},{5,4},{6,7},{7,6},{8,9},{9,8},{10,11... | collective-permute-start | bytes 1081352 | tf_op jit(solution)/shard_map/ppermute | solution.py:252
  100.8 17.7 %collective-permute-start.10 = (f32[176,512]{1,0:T(8,128)S(1)}, f32[176,512]{1,0:T(8,128)S(1)}, u32[]{:S(2)}, u32[]{:S(2)}) collective-permute-start(f32[176,512]{1,0:T(8,128)S(1)} %add.10), channel_id=1, source_target_pairs={{0,2},{2,0},{1,3},{3,1},{4,6},{6,4},{5,7},{7,5},{8,10},{10,8},{9,1... | collective-permute-start | bytes 1081352 | tf_op jit(solution)/shard_map/ppermute | solution.py:252
  105.6 11.2 %collective-permute-start = (bf16[208,256]{1,0:T(8,128)(2,1)S(1)}, bf16[208,256]{1,0:T(8,128)(2,1)S(1)}, u32[]{:S(2)}, u32[]{:S(2)}) collective-permute-start(bf16[208,256]{1,0:T(8,128)(2,1)S(1)} %get-tuple-element.9), channel_id=1, source_target_pairs={{0,2},{2,0},{1,3},{3,1},{4,6},{6,4},{5,7},{7,5},{8,10},{10,8},{9,1... | collective-permute-start | bytes 319496 | tf_op jit(solution)/shard_map/ppermute | solution.py:252
